TPU v7x, 128 devices: a whole 4x4x4 slice. The times are simulated.
128 devices in a mesh: lat: 8 (over x, core), lon: 16 (over z, y).
Axes of the slice: x: 4, y: 4, z: 4, core: 2. Of those that a mesh axis runs over, the one named last changes fastest.
Arguments:
- mesh_nodes: bfloat16 [32768, 512], P(('lat', 'lon')), may hold values from -6 to 6
- mesh_edges: bfloat16 [262144, 512], P(('lat', 'lon')), may hold values from -6 to 6
- grid_state: bfloat16 [256, 512, 512], P('lat', 'lon'), may hold values from -6 to 6
- decoder_edges: bfloat16 [3, 256, 512, 512], P(None, 'lat', 'lon'), may hold values from -6 to 6
- edge_send: int32 [262144], P(('lat', 'lon')), may hold values from 0 to 1279
- edge_recv: int32 [262144], P(('lat', 'lon')), may hold values from -1 to 255, as said below
- halo_lists: int32 [128, 128, 8], P(('lat', 'lon')), may hold values from 0 to 255
- decoder_lists: int32 [128, 128, 4], P(('lat', 'lon')), may hold values from 0 to 255
- decoder_sources: int32 [3, 256, 512], P(None, 'lat', 'lon'), may hold values from 0 to 511
- edge_first: bfloat16 [2, 1536, 512], replicated, may hold values from -0.15625 to 0.15625
- edge_second: bfloat16 [2, 512, 512], replicated, may hold values from -0.25 to 0.25
- node_first: bfloat16 [2, 1024, 512], replicated, may hold values from -0.1875 to 0.1875
- node_second: bfloat16 [2, 512, 512], replicated, may hold values from -0.25 to 0.25
- decoder_first: bfloat16 [1536, 512], replicated, may hold values from -0.15625 to 0.15625
- decoder_second: bfloat16 [512, 512], replicated, may hold values from -0.25 to 0.25
- grid_first: bfloat16 [1024, 512], replicated, may hold values from -0.1875 to 0.1875
- grid_second: bfloat16 [512, 512], replicated, may hold values from -0.25 to 0.25
Outputs:
- mesh_final: bfloat16 [32768, 512], P(('lat', 'lon'))
- grid_final: bfloat16 [256, 512, 512], P('lat', 'lon')
Inputs may be any that keep to these rules, and one draw needn't show every extreme that they name: `edge_recv`: on each partition the live edges come first; their number is a multiple of 128, at least 128 and at most 2048, and some partition has 2048; live receivers are local node rows, padding slots hold -1.
All inputs are finite; a program needn't handle non-finite values.
Results may differ from a plain program's by a relative error of at most 0.012.
Values may be sent and summed in bfloat16 or wider, within the bound.
No kernel may reach another device: no remote copies, remote signals or barrier semaphores. Data moves between devices by JAX's collectives and lax.ppermute only.
A program may use at most 128 MiB of HBM per device.

v0:
```python
import jax
import jax.numpy as jnp
from jax import lax
from jax.sharding import PartitionSpec as P

epsilon = 1e-05


def normalize(values):
    average = jnp.mean(values, axis=-1, keepdims=True)
    centered = values - average
    spread = jnp.mean(centered * centered, axis=-1, keepdims=True)
    return centered * lax.rsqrt(spread + epsilon)


def perceptron(inputs, layer_one, layer_two):
    hidden = jax.nn.silu(jnp.dot(inputs, layer_one, preferred_element_type=jnp.float32)).astype(
        jnp.bfloat16
    )
    return normalize(jnp.dot(hidden, layer_two, preferred_element_type=jnp.float32))


def pick_rows(indices, lookup):
    table_rows = lookup.shape[0]
    picker = (indices[:, None] == jnp.arange(table_rows, dtype=jnp.int32)[None, :]).astype(
        jnp.bfloat16
    )
    return (
        picker,
        jnp.dot(picker, lookup, preferred_element_type=jnp.float32).astype(jnp.bfloat16),
    )


def mesh_route(outgoing):
    return lax.all_to_all(outgoing, ("lat", "lon"), split_axis=0, concat_axis=0, tiled=True)


def decoder_route(outgoing):
    return lax.all_to_all(outgoing, ("lat", "lon"), split_axis=0, concat_axis=0, tiled=True)


def mesh_layer(
    nodes_now, edges_now, edge_send, edge_recv, send_lists, w_edge1, w_edge2, w_node1, w_node2
):
    node_count, feature_width = nodes_now.shape
    flat_rows = send_lists.reshape(-1)
    ignored, outgoing = pick_rows(flat_rows, nodes_now)
    outgoing = outgoing.reshape(send_lists.shape[1], send_lists.shape[2], feature_width)
    incoming = mesh_route(outgoing).reshape(-1, feature_width)
    lookup = jnp.concatenate([nodes_now, incoming], axis=0)
    edge_count = edges_now.shape[0]
    block_rows = 512
    live_edges = jnp.sum((edge_recv >= 0).astype(jnp.int32))
    block_count = (live_edges + block_rows - 1) // block_rows

    def mesh_advance(number, carry):
        summed, updated = carry
        first_row = number * block_rows
        edge_block = lax.dynamic_slice_in_dim(edges_now, first_row, block_rows, 0)
        senders = lax.dynamic_slice_in_dim(edge_send, first_row, block_rows, 0)
        targets = lax.dynamic_slice_in_dim(edge_recv, first_row, block_rows, 0)
        ignored_send, from_send = pick_rows(senders, lookup)
        pick_recv, from_recv = pick_rows(targets, nodes_now)
        result = perceptron(
            jnp.concatenate([edge_block, from_send, from_recv], axis=1), w_edge1, w_edge2
        )
        message = result.astype(jnp.bfloat16)
        summed = summed + lax.dot_general(
            pick_recv, message, (((0,), (0,)), ((), ())), preferred_element_type=jnp.float32
        )
        fresh = (edge_block.astype(jnp.float32) + result).astype(jnp.bfloat16)
        updated = lax.dynamic_update_slice_in_dim(updated, fresh, first_row, 0)
        return (summed, updated)

    start_sum = jnp.zeros((node_count, feature_width), jnp.float32)
    summed, fresh_edges = lax.fori_loop(0, block_count, mesh_advance, (start_sum, edges_now))
    gathered = summed.astype(jnp.bfloat16)
    result = perceptron(jnp.concatenate([nodes_now, gathered], axis=1), w_node1, w_node2)
    fresh_nodes = (nodes_now.astype(jnp.float32) + result).astype(jnp.bfloat16)
    return (fresh_nodes, fresh_edges)


def decode(
    nodes_now,
    grid_state,
    decoder_edges,
    decoder_sources,
    decoder_lists,
    decoder_first,
    decoder_second,
    grid_first,
    grid_second,
):
    feature_width = nodes_now.shape[1]
    ignored, outgoing = pick_rows(decoder_lists.reshape(-1), nodes_now)
    outgoing = outgoing.reshape(decoder_lists.shape[1], decoder_lists.shape[2], feature_width)
    lookup = decoder_route(outgoing).reshape(-1, feature_width)
    tile_lat, tile_lon = (grid_state.shape[0], grid_state.shape[1])
    cells = tile_lat * tile_lon
    flat_grid = grid_state.reshape(cells, feature_width)
    flat_edges = decoder_edges.reshape(3, cells, feature_width)
    flat_sources = decoder_sources.reshape(3, cells)
    block_rows = 512

    def decode_advance(number, updated):
        first_row = number * block_rows
        grid_block = lax.dynamic_slice_in_dim(flat_grid, first_row, block_rows, 0)
        summed = jnp.zeros((block_rows, feature_width), jnp.float32)
        for branch in range(3):
            sources = lax.dynamic_slice_in_dim(flat_sources[branch], first_row, block_rows, 0)
            ignored_pick, mesh_rows = pick_rows(sources, lookup)
            edge_block = lax.dynamic_slice_in_dim(flat_edges[branch], first_row, block_rows, 0)
            result = perceptron(
                jnp.concatenate([edge_block, mesh_rows, grid_block], axis=1),
                decoder_first,
                decoder_second,
            )
            summed = summed + lax.optimization_barrier(result.astype(jnp.bfloat16)).astype(
                jnp.float32
            )
        gathered = summed.astype(jnp.bfloat16)
        result = perceptron(
            jnp.concatenate([grid_block, gathered], axis=1), grid_first, grid_second
        )
        fresh = (grid_block.astype(jnp.float32) + result).astype(jnp.bfloat16)
        return lax.dynamic_update_slice_in_dim(updated, fresh, first_row, 0)

    decoded = lax.fori_loop(0, cells // block_rows, decode_advance, flat_grid)
    return decoded.reshape(tile_lat, tile_lon, feature_width)


def shards(
    mesh_nodes,
    mesh_edges,
    grid_state,
    decoder_edges,
    edge_send,
    edge_recv,
    halo_lists,
    decoder_lists,
    decoder_sources,
    edge_first,
    edge_second,
    node_first,
    node_second,
    decoder_first,
    decoder_second,
    grid_first,
    grid_second,
):
    nodes_now, edges_now = (mesh_nodes, mesh_edges)
    for layer in range(edge_first.shape[0]):
        nodes_now, edges_now = mesh_layer(
            nodes_now,
            edges_now,
            edge_send,
            edge_recv,
            halo_lists,
            edge_first[layer],
            edge_second[layer],
            node_first[layer],
            node_second[layer],
        )
    grid_final = decode(
        nodes_now,
        grid_state,
        decoder_edges,
        decoder_sources,
        decoder_lists,
        decoder_first,
        decoder_second,
        grid_first,
        grid_second,
    )
    return (nodes_now, grid_final)


def solution(mesh):
    placed = (
        P(("lat", "lon"), None),
        P(("lat", "lon"), None),
        P("lat", "lon", None),
        P(None, "lat", "lon", None),
        P(("lat", "lon")),
        P(("lat", "lon")),
        P(("lat", "lon"), None, None),
        P(("lat", "lon"), None, None),
        P(None, "lat", "lon"),
        P(),
        P(),
        P(),
        P(),
        P(),
        P(),
        P(),
        P(),
    )
    return jax.shard_map(
        shards,
        mesh=mesh,
        in_specs=placed,
        out_specs=(P(("lat", "lon"), None), P("lat", "lon", None)),
        check_vma=False,
    )
```

profile of v0, /device:TPU:1, one launch (start us, length us, event | category | flops | bytes accessed | tf_op | source)
XLA Modules:
  0.0 254.2 jit_solution(9361505626225935795)
XLA Ops:
  1.5 2.6 %fusion.92 = bf16[128,8,512]{2,1,0:T(8,128)(2,1)} fusion(bf16[256,512]{1,0:T(8,128)(2,1)} %param.23, s32[1024]{0:T(1024)S(1)} %eq.196), kind=kOutput, calls=%fused_computation.135 | convolution fusion | flops 269221888 | bytes 1314816 | tf_op jit(solution)/shard_map/dot_general | solution.py:30
  4.1 11.5 %all-to-all-start = ((bf16[128,8,512]{2,1,0:T(8,128)(2,1)}), bf16[128,8,512]{2,1,0:T(8,128)(2,1)S(1)}, u32[]{:S(2)}, u32[]{:S(2)}) async-start(bf16[128,8,512]{2,1,0:T(8,128)(2,1)} %fusion.92), calls=%async_computation | async-start | bytes 2097152 | tf_op jit(solution)/shard_map/all_to_all | solution.py:35
  16.9 2.5 copy.26
  19.4 2.3 slice_bitcast_fusion.2
  21.7 3.8 %slice_bitcast_fusion = (bf16[1536,512]{1,0:T(8,128)(2,1)}, bf16[1536,512]{1,0:T(8,128)(2,1)}) fusion(bf16[2,1536,512]{2,1,0:T(8,128)(2,1)} %param.32), kind=kLoop, calls=%fused_computation.131 | loop fusion | bytes 6291456 | tf_op jit(solution)/shard_map/squeeze | solution.py:159
  25.5 9.0 %all-to-all-done = bf16[128,8,512]{2,1,0:T(8,128)(2,1)S(1)} async-done(((bf16[128,8,512]{2,1,0:T(8,128)(2,1)}), bf16[128,8,512]{2,1,0:T(8,128)(2,1)S(1)}, u32[]{:S(2)}, u32[]{:S(2)}) %all-to-all-start) | async-done | bytes 1048608 | tf_op jit(solution)/shard_map/all_to_all | solution.py:35
  35.7 10.1 %while.37 = (s32[]{:T(128)}, f32[256,512]{1,0:T(8,128)S(1)}, bf16[2048,512]{0,1:T(8,128)(2,1)}, s32[]{:T(128)}, s32[2048]{0:T(1024)S(1)}, /*index=5*/bf16[2048,5...) while((s32[]{:T(128)}, f32[256,512]{1,0:T(8,128)S(1)}, ...), condition=%wide.region_4.5_spmd, body=%wide.region_1.4_spmd.sunk | while | flops 2024145408 | bytes 16814320 | solution.py:76
  36.4 3.1 %fusion.226 = bf16[512,512]{0,1:T(8,128)(2,1)} fusion(bf16[1280,512]{1,0:T(8,128)(2,1)} %get-tuple-element.731, s32[512]{0:T(512)S(1)} %dynamic_slice.86), kind=kOutput, calls=%fused_computation.10.clone.1 | convolution fusion | flops 672006144 | bytes 1837056 | tf_op jit(solution)/shard_map/while/body/dot_general | solution.py:30
  40.9 3.2 %fusion.227 = (f32[512]{0:T(512)S(1)}, f32[512,512]{0,1:T(8,128)S(1)}) fusion(bf16[512,512]{1,0:T(8,128)(2,1)S(1)} %copy-done.14, bf16[1536,512]{1,0:T(8,128)(2,1)} %get-tuple-element.733, bf16[512,512]{0,1:T(8,128)(2,1)S(1)} %convolution_convert_fusion.13, bf16[512,512]{0,1:T(8,128)(2,1)} %fusion.226, bf16[512,512]{0,1:T(8,128)(2,1)S(1)} %copy.43), kind=kOutput, calls=%fused_computation.182.clone.1 | convolution fusion | flops 1080032768 | bytes 4720640 | tf_op jit(solution)/shard_map/while/body/dot_general | solution.py:20
  45.8 2.1 fusion.153
  49.8 34.2 %all-to-all-start.1 = ((bf16[128,8,512]{2,1,0:T(8,128)(2,1)}), bf16[128,8,512]{2,1,0:T(8,128)(2,1)S(1)}, u32[]{:S(2)}, u32[]{:S(2)}) async-start(bf16[128,8,512]{2,1,0:T(8,128)(2,1)} %fusion.93), calls=%async_computation.1 | async-start | bytes 2097152 | tf_op jit(solution)/shard_map/all_to_all | solution.py:35
  84.3 18.7 %all-to-all-done.1 = bf16[128,8,512]{2,1,0:T(8,128)(2,1)S(1)} async-done(((bf16[128,8,512]{2,1,0:T(8,128)(2,1)}), bf16[128,8,512]{2,1,0:T(8,128)(2,1)S(1)}, u32[]{:S(2)}, u32[]{:S(2)}) %all-to-all-start.1) | async-done | bytes 1048608 | tf_op jit(solution)/shard_map/all_to_all | solution.py:35
  104.1 8.8 %while.38 = (s32[]{:T(128)}, f32[256,512]{1,0:T(8,128)S(1)}, s32[]{:T(128)}, s32[2048]{0:T(1024)S(1)}, bf16[2048,512]{0,1:T(8,128)(2,1)}, /*index=5*/s32[2048]{0...) while((s32[]{:T(128)}, f32[256,512]{1,0:T(8,128)S(1)}, ...), condition=%wide.region_10.11_spmd, body=%wide.region_7.10_spmd.sunk | while | flops 2022834688 | bytes 12615879 | solution.py:76
  104.7 3.0 %fusion.235 = bf16[512,512]{1,0:T(8,128)(2,1)} fusion(bf16[1280,512]{1,0:T(8,128)(2,1)} %get-tuple-element.773, s32[512]{0:T(512)S(1)} %dynamic_slice.89), kind=kOutput, calls=%fused_computation.40.clone.1 | convolution fusion | flops 672006144 | bytes 1837056 | tf_op jit(solution)/shard_map/while/body/dot_general | solution.py:30
  109.0 3.1 %fusion.236 = (f32[512]{0:T(512)S(1)}, f32[512,512]{0,1:T(8,128)S(1)}) fusion(bf16[512,512]{1,0:T(8,128)(2,1)S(1)} %get-tuple-element.776, bf16[1536,512]{1,0:T(8,128)(2,1)} %get-tuple-element.775, bf16[512,512]{1,0:T(8,128)(2,1)S(1)} %convolution_convert_fusion.14, bf16[512,512]{1,0:T(8,128)(2,1)} %fusion.235, bf16[512,512]{1,0:T(8,128)(2,1)S(1)} %copy.44), kind=kOutput, calls=%fused_computation.183.clone.1 | convolution fusion | flops 1080032768 | bytes 4720640 | tf_op jit(solution)/shard_map/while/body/dot_general | solution.py:20
  113.0 2.2 fusion.158
  116.9 30.6 %all-to-all-start.2 = ((bf16[128,4,512]{2,1,0:T(4,128)(2,1)}), bf16[128,4,512]{2,1,0:T(4,128)(2,1)}, u32[]{:S(2)}, u32[]{:S(2)}) async-start(bf16[128,4,512]{2,1,0:T(4,128)(2,1)} %reshape.177), calls=%async_computation.2 | async-start | bytes 1048576 | tf_op jit(solution)/shard_map/all_to_all | solution.py:39
  148.5 3.2 %copy.32 = bf16[3,1024,512]{1,2,0:T(8,128)(2,1)S(1)} copy(bf16[3,1024,512]{2,1,0:T(8,128)(2,1)} %bitcast.128) | data formatting | bytes 6291456 | tf_op jit(solution)/shard_map/while | solution.py:128
  151.8 9.4 %all-to-all-done.2 = bf16[128,4,512]{2,1,0:T(4,128)(2,1)} async-done(((bf16[128,4,512]{2,1,0:T(4,128)(2,1)}), bf16[128,4,512]{2,1,0:T(4,128)(2,1)}, u32[]{:S(2)}, u32[]{:S(2)}) %all-to-all-start.2) | async-done | bytes 524320 | tf_op jit(solution)/shard_map/all_to_all | solution.py:39
  161.2 2.0 reshape.178
  163.2 91.0 %while.39 = (s32[]{:T(128)}, bf16[1024,512]{1,0:T(8,128)(2,1)}, bf16[1024,512]{1,0:T(8,128)(2,1)}, bf16[3,1024,512]{1,2,0:T(8,128)(2,1)S(1)}, s32[3,1024]{1,0:T(...) while((s32[]{:T(128)}, bf16[1024,512]{1,0:T(8,128)(2,1)}, ...), condition=%wide.region_22.23_spmd, body=%wide.region_13.22_spmd.sunk | while | flops 4864346112 | bytes 77187544 | solution.py:128
  163.2 1.9 constant_dynamic-slice_fusion.13
  165.0 2.1 copy.45
  167.1 2.5 convolution_convert_fusion.15
  172.0 4.6 %fusion.251 = (f32[512]{0:T(512)S(1)}, f32[512,512]{0,1:T(8,128)}) fusion(bf16[512,512]{1,0:T(8,128)(2,1)} %get-tuple-element.816, bf16[1536,512]{1,0:T(8,128)(2,1)} %get-tuple-element.815, bf16[512,512]{0,1:T(8,128)(2,1)} %copy.45, bf16[512,512]{0,1:T(8,128)(2,1)} %convolution_convert_fusion.15, bf16[512,512]{0,1:T(8,128)(2,1)} %get-tuple-element.681), kind=kOutput, calls=%fused_computation.186.clone.1 | convolution fusion | flops 1080032768 | bytes 4720640 | tf_op jit(solution)/shard_map/while/body/eval_jaxpr/dot_general | solution.py:20
  176.6 1.5 multiply_reduce_fusion.16
  180.5 4.6 %fusion.252 = (f32[512]{0:T(512)S(1)}, f32[512,512]{0,1:T(8,128)}) fusion(bf16[512,512]{1,0:T(8,128)(2,1)} %get-tuple-element.816, bf16[1536,512]{1,0:T(8,128)(2,1)} %get-tuple-element.815, bf16[512,512]{0,1:T(8,128)(2,1)} %copy.45, bf16[512,512]{0,1:T(8,128)(2,1)} %convolution_convert_fusion.16, bf16[512,512]{0,1:T(8,128)(2,1)} %get-tuple-element.685), kind=kOutput, calls=%fused_computation.187.clone.1 | convolution fusion | flops 1080032768 | bytes 4720640 | tf_op jit(solution)/shard_map/while/body/eval_jaxpr/dot_general | solution.py:20
  185.1 1.5 multiply_reduce_fusion.17
  189.8 4.5 %fusion.253 = (f32[512]{0:T(512)S(1)}, f32[512,512]{0,1:T(8,128)}) fusion(bf16[512,512]{1,0:T(8,128)(2,1)} %get-tuple-element.816, bf16[1536,512]{1,0:T(8,128)(2,1)} %get-tuple-element.815, bf16[512,512]{0,1:T(8,128)(2,1)} %copy.45, bf16[512,512]{0,1:T(8,128)(2,1)} %convolution_convert_fusion.17, bf16[512,512]{0,1:T(8,128)(2,1)} %dynamic-slice_bitcast_fusion.6), kind=kOutput, calls=%fused_computation.188.clone.1 | convolution fusion | flops 1080032768 | bytes 4720640 | tf_op jit(solution)/shard_map/while/body/eval_jaxpr/dot_general | solution.py:20
  194.4 1.5 multiply_reduce_fusion.18
  197.2 4.0 %fusion.254 = (f32[512]{0:T(512)S(1)}, f32[512,512]{0,1:T(8,128)}) fusion(bf16[512,512]{1,0:T(8,128)(2,1)} %get-tuple-element.818, bf16[1024,512]{1,0:T(8,128)(2,1)} %get-tuple-element.817, bf16[512,512]{0,1:T(8,128)(2,1)} %add_convert_fusion.7, bf16[512,512]{0,1:T(8,128)(2,1)} %copy.45), kind=kOutput, calls=%fused_computation.189.clone.1 | convolution fusion | flops 808975872 | bytes 3672064 | tf_op jit(solution)/shard_map/while/body/eval_jaxpr/dot_general | solution.py:20
  202.7 2.0 add_convert_fusion.8
  204.8 2.0 copy.46
  206.8 1.9 constant_dynamic-update-slice_fusion.2
  208.7 1.9 constant_dynamic-slice_fusion.13
  210.5 2.1 copy.45
  212.6 2.5 convolution_convert_fusion.15
  217.5 4.6 %fusion.251 = (f32[512]{0:T(512)S(1)}, f32[512,512]{0,1:T(8,128)}) fusion(bf16[512,512]{1,0:T(8,128)(2,1)} %get-tuple-element.816, bf16[1536,512]{1,0:T(8,128)(2,1)} %get-tuple-element.815, bf16[512,512]{0,1:T(8,128)(2,1)} %copy.45, bf16[512,512]{0,1:T(8,128)(2,1)} %convolution_convert_fusion.15, bf16[512,512]{0,1:T(8,128)(2,1)} %get-tuple-element.681), kind=kOutput, calls=%fused_computation.186.clone.1 | convolution fusion | flops 1080032768 | bytes 4720640 | tf_op jit(solution)/shard_map/while/body/eval_jaxpr/dot_general | solution.py:20
  222.1 1.5 multiply_reduce_fusion.16
  226.0 4.6 %fusion.252 = (f32[512]{0:T(512)S(1)}, f32[512,512]{0,1:T(8,128)}) fusion(bf16[512,512]{1,0:T(8,128)(2,1)} %get-tuple-element.816, bf16[1536,512]{1,0:T(8,128)(2,1)} %get-tuple-element.815, bf16[512,512]{0,1:T(8,128)(2,1)} %copy.45, bf16[512,512]{0,1:T(8,128)(2,1)} %convolution_convert_fusion.16, bf16[512,512]{0,1:T(8,128)(2,1)} %get-tuple-element.685), kind=kOutput, calls=%fused_computation.187.clone.1 | convolution fusion | flops 1080032768 | bytes 4720640 | tf_op jit(solution)/shard_map/while/body/eval_jaxpr/dot_general | solution.py:20
  230.6 1.5 multiply_reduce_fusion.17
  235.4 4.5 %fusion.253 = (f32[512]{0:T(512)S(1)}, f32[512,512]{0,1:T(8,128)}) fusion(bf16[512,512]{1,0:T(8,128)(2,1)} %get-tuple-element.816, bf16[1536,512]{1,0:T(8,128)(2,1)} %get-tuple-element.815, bf16[512,512]{0,1:T(8,128)(2,1)} %copy.45, bf16[512,512]{0,1:T(8,128)(2,1)} %convolution_convert_fusion.17, bf16[512,512]{0,1:T(8,128)(2,1)} %dynamic-slice_bitcast_fusion.6), kind=kOutput, calls=%fused_computation.188.clone.1 | convolution fusion | flops 1080032768 | bytes 4720640 | tf_op jit(solution)/shard_map/while/body/eval_jaxpr/dot_general | solution.py:20
  239.9 1.5 multiply_reduce_fusion.18
  242.8 4.0 %fusion.254 = (f32[512]{0:T(512)S(1)}, f32[512,512]{0,1:T(8,128)}) fusion(bf16[512,512]{1,0:T(8,128)(2,1)} %get-tuple-element.818, bf16[1024,512]{1,0:T(8,128)(2,1)} %get-tuple-element.817, bf16[512,512]{0,1:T(8,128)(2,1)} %add_convert_fusion.7, bf16[512,512]{0,1:T(8,128)(2,1)} %copy.45), kind=kOutput, calls=%fused_computation.189.clone.1 | convolution fusion | flops 808975872 | bytes 3672064 | tf_op jit(solution)/shard_map/while/body/eval_jaxpr/dot_general | solution.py:20
  246.7 1.5 multiply_reduce_fusion.19
  248.3 2.0 add_convert_fusion.8
  250.3 2.0 copy.46
  252.3 1.9 constant_dynamic-update-slice_fusion.2
  (140 shorter events, 35.4 us)
Async XLA Ops:
  1.5 14.1 %copy-start.15 = (s32[2048]{0:T(1024)S(1)}, s32[2048]{0:T(1024)}, u32[]{:S(2)}) copy-start(s32[2048]{0:T(1024)} %param.28) | copy-start | bytes 24580
  1.5 15.4 %copy-start.9 = (bf16[2048,512]{1,0:T(8,128)(2,1)S(1)}, bf16[2048,512]{1,0:T(8,128)(2,1)}, u32[]{:S(2)}) copy-start(bf16[2048,512]{1,0:T(8,128)(2,1)} %param.24) | copy-start | bytes 6291460
  4.1 30.4 %all-to-all-start = ((bf16[128,8,512]{2,1,0:T(8,128)(2,1)}), bf16[128,8,512]{2,1,0:T(8,128)(2,1)S(1)}, u32[]{:S(2)}, u32[]{:S(2)}) async-start(bf16[128,8,512]{2,1,0:T(8,128)(2,1)} %fusion.92), calls=%async_computation | async-start | bytes 2097152 | tf_op jit(solution)/shard_map/all_to_all | solution.py:35
  21.6 12.8 %copy-start.7 = (bf16[256,512]{1,0:T(8,128)(2,1)S(1)}, bf16[256,512]{1,0:T(8,128)(2,1)}, u32[]{:S(2)}) copy-start(bf16[256,512]{1,0:T(8,128)(2,1)} %param.23) | copy-start | bytes 786436
  34.5 1.2 copy-start.16
  39.5 1.4 copy-start.14
  48.4 35.7 %copy-start.18 = (s32[1,128,4]{1,2,0:T(4,128)S(1)}, s32[1,128,4]{1,2,0:T(4,128)}, u32[]{:S(2)}) copy-start(s32[1,128,4]{1,2,0:T(4,128)} %param.30) | copy-start | bytes 6148
  49.8 53.1 %all-to-all-start.1 = ((bf16[128,8,512]{2,1,0:T(8,128)(2,1)}), bf16[128,8,512]{2,1,0:T(8,128)(2,1)S(1)}, u32[]{:S(2)}, u32[]{:S(2)}) async-start(bf16[128,8,512]{2,1,0:T(8,128)(2,1)} %fusion.93), calls=%async_computation.1 | async-start | bytes 2097152 | tf_op jit(solution)/shard_map/all_to_all | solution.py:35
  102.9 1.2 copy-start.13
  115.6 32.9 %copy-start.10 = (bf16[256,512]{1,0:T(8,128)(2,1)}, bf16[256,512]{1,0:T(8,128)(2,1)S(1)}, u32[]{:S(2)}) copy-start(bf16[256,512]{1,0:T(8,128)(2,1)S(1)} %add_convert_fusion.3) | copy-start | bytes 786436
  115.6 31.9 %copy-start.8 = (bf16[32,32,512]{2,1,0:T(8,128)(2,1)S(1)}, bf16[32,32,512]{2,1,0:T(8,128)(2,1)}, u32[]{:S(2)}) copy-start(bf16[32,32,512]{2,1,0:T(8,128)(2,1)} %param.25) | copy-start | bytes 3145732
  116.9 44.3 %all-to-all-start.2 = ((bf16[128,4,512]{2,1,0:T(4,128)(2,1)}), bf16[128,4,512]{2,1,0:T(4,128)(2,1)}, u32[]{:S(2)}, u32[]{:S(2)}) async-start(bf16[128,4,512]{2,1,0:T(4,128)(2,1)} %reshape.177), calls=%async_computation.2 | async-start | bytes 1048576 | tf_op jit(solution)/shard_map/all_to_all | solution.py:39
  148.5 3.2 %copy-start.17 = (s32[3,32,32]{2,1,0:T(8,128)S(1)}, s32[3,32,32]{2,1,0:T(8,128)}, u32[]{:S(2)}) copy-start(s32[3,32,32]{2,1,0:T(8,128)} %param.31) | copy-start | bytes 36868
  176.6 1.5 copy-start
  176.6 2.5 copy-start.11
  185.1 1.5 copy-start.1
  185.1 2.5 copy-start.12
  186.6 2.4 copy-start.4
  194.4 1.6 copy-start.2
  194.4 1.7 copy-start.5
  194.4 1.8 copy-start.6
  201.2 1.5 copy-start.3
  222.1 1.5 copy-start
  222.1 2.5 copy-start.11
  230.6 1.5 copy-start.1
  230.6 2.5 copy-start.12
  232.1 2.4 copy-start.4
  239.9 1.6 copy-start.2
  239.9 1.7 copy-start.5
  239.9 1.8 copy-start.6
  246.7 1.5 copy-start.3
where the time goes:
time: 257 us; the launch traced here: 254 us
  starting transfers between devices  76.3 us (30%)
  matrix products  68.9 us (27%)
  local copies, waits for them, and re-layouts  42.6 us (17%)
  waiting for transfers between devices  37.1 us (14%)
  other arithmetic  27.3 us (11%)
    dot_general x12, matrix products, perceptron(): jnp.dot(hidden, layer_two, preferred_element_type=jnp.float32)  45.9 us
    all_to_all x2, starting transfers between devices, mesh_route(): lax.all_to_all(outgoing, ('lat', 'lon'), split_axis=0, concat_axis=0, til...  45.7 us
    all_to_all x1, starting transfers between devices, decoder_route(): lax.all_to_all(outgoing, ('lat', 'lon'), split_axis=0, concat_axis=0, til...  30.6 us
    all_to_all x2, waiting for transfers between devices, mesh_route(): lax.all_to_all(outgoing, ('lat', 'lon'), split_axis=0, concat_axis=0, til...  27.7 us
    dot_general x13, matrix products, pick_rows(): jnp.dot(picker, lookup, preferred_element_type=jnp.float32)  22 us
    reduce_sum x12, other arithmetic, normalize(): spread = jnp.mean(centered * centered, axis=-1, keepdims=True)  12.7 us
    all_to_all x1, waiting for transfers between devices, decoder_route(): lax.all_to_all(outgoing, ('lat', 'lon'), split_axis=0, concat_axis=0, til...  9.42 us
    dynamic_slice x4, local copies, waits for them, and re-layouts, decode_advance(): grid_block = lax.dynamic_slice_in_dim(flat_grid, first_row, block_rows, 0)  7.85 us
  transfers between devices with their start and end apart: 3, of which 3 were waited for; matrix products, arithmetic and copies ran while one was open for 5% of the time, Pallas kernels for 0%

commit v1 on v0

v1 whole, which is shorter than its diff:
```python
import functools

import jax
import jax.numpy as jnp
from jax import lax
from jax.experimental import pallas as pl
from jax.experimental.pallas import tpu as pltpu
from jax.sharding import PartitionSpec as P

epsilon = 1e-05
BLOCK = 512
CELLS = 256
GRANT = 62 << 20
bf16 = jnp.bfloat16
f32 = jnp.float32
HBM = pltpu.HBM
VMEM = pltpu.VMEM


def dot(a, b):
    return jnp.dot(a, b, preferred_element_type=f32)


def silu(values):
    half = values * 0.5
    return half + half * jnp.tanh(half)


def normalize(values):
    average = jnp.mean(values, axis=-1, keepdims=True)
    centered = values - average
    spread = jnp.mean(centered * centered, axis=-1, keepdims=True)
    return centered * lax.rsqrt(spread + epsilon)


def tail(before, second):
    return normalize(dot(silu(before).astype(bf16), second))


def picker_rows(row, table_rows, first):
    spread = jnp.broadcast_to(row.astype(f32), (128, 128)).T
    lanes = lax.broadcasted_iota(jnp.int32, (128, 128), 1).astype(f32)
    shifted = spread - lanes
    pieces = [
        jnp.where(shifted == float(first + c * 128), 1.0, 0.0).astype(bf16)
        for c in range(table_rows // 128)
    ]
    return jnp.concatenate(pieces, axis=1)


def fill_picker(oh_ref, idx_ref, first_index_row, rows, table_rows, first):
    for r in range(rows // 128):
        row = idx_ref[pl.ds(first_index_row + r, 1), :]
        oh_ref[r * 128 : (r + 1) * 128, :] = picker_rows(row, table_rows, first)


def pick_kernel(lists, nodes, out, oh):
    fill_picker(oh, lists, 0, out.shape[0], nodes.shape[0], 0)
    out[...] = dot(oh[...], nodes[...]).astype(bf16)


def pick_first(lists, nodes):
    rows = lists.shape[0] * 128
    return pl.pallas_call(
        pick_kernel,
        out_shape=jax.ShapeDtypeStruct((rows, nodes.shape[1]), bf16),
        in_specs=[pl.BlockSpec(memory_space=VMEM)] * 2,
        out_specs=pl.BlockSpec(memory_space=VMEM),
        scratch_shapes=[VMEM((rows, nodes.shape[0]), bf16)],
        compiler_params=pltpu.CompilerParams(vmem_limit_bytes=GRANT),
        cost_estimate=pl.CostEstimate(
            flops=2 * rows * nodes.shape[0] * nodes.shape[1], bytes_accessed=1 << 20, transcendentals=0
        ),
        name="pick_first",
    )(lists, nodes)


def before_kernel(live, edges, send, recv, nodes, first, out, oh):
    block = pl.program_id(0)
    width = nodes.shape[1]
    count = nodes.shape[0]

    @pl.when(block < live[0])
    def _():
        rows = edges.shape[0]
        steps = rows // 128
        fill_picker(oh, send, block * steps, rows, count, 0)
        from_send = dot(oh[...], nodes[...]).astype(bf16)
        total = dot(edges[...], first[0, :width, :]) + dot(from_send, first[0, width : 2 * width, :])
        fill_picker(oh, recv, block * steps, rows, count, 0)
        from_recv = dot(oh[...], nodes[...]).astype(bf16)
        out[...] = total + dot(from_recv, first[0, 2 * width :, :])


def edges_before(live, edges, send, recv, nodes, edge_first, layer):
    count, width = edges.shape
    blocks = count // BLOCK
    clamp = lambda i, live: (jnp.minimum(i, live[0] - 1), 0)
    whole = lambda i, live: (0, 0)
    grid_spec = pltpu.PrefetchScalarGridSpec(
        num_scalar_prefetch=1,
        grid=(blocks,),
        in_specs=[
            pl.BlockSpec((BLOCK, width), clamp),
            pl.BlockSpec(send.shape, whole),
            pl.BlockSpec(recv.shape, whole),
            pl.BlockSpec(nodes.shape, whole),
            pl.BlockSpec((1, 3 * width, width), lambda i, live: (layer, 0, 0)),
        ],
        out_specs=pl.BlockSpec((BLOCK, width), clamp),
        scratch_shapes=[VMEM((BLOCK, nodes.shape[0]), bf16)],
    )
    return pl.pallas_call(
        before_kernel,
        grid_spec=grid_spec,
        out_shape=jax.ShapeDtypeStruct((count, width), f32),
        compiler_params=pltpu.CompilerParams(vmem_limit_bytes=GRANT),
        cost_estimate=pl.CostEstimate(flops=8 * count * width * width, bytes_accessed=8 << 20, transcendentals=0),
        name=f"edges_before_{layer}",
    )(live, edges, send, recv, nodes, edge_first)


def layer_kernel(
    layer,
    last,
    live,
    send,
    recv_rows,
    lists,
    incoming,
    before,
    edges,
    nodes,
    edge_first,
    edge_second,
    node_first,
    node_second,
    *rest,
):
    if last:
        nodes_out, outgoing = rest[:2]
        rest = rest[2:]
        fresh_out = fresh = out_sem = edge_buf = None
    else:
        nodes_out, outgoing, fresh_out = rest[:3]
        rest = rest[3:]
        edge_buf, fresh, out_sem = rest[:3]
        rest = rest[3:]
    send_buf, before_buf, second_buf, node_buf, nf_buf, ns_buf, table, oh, oh_lists, acc, sem, bsem = rest
    width = nodes.shape[1]
    count = nodes.shape[0]
    blocks = before.shape[0] // BLOCK
    live_blocks = live[0]

    def copy(src, dst, which):
        return pltpu.make_async_copy(src, dst, sem.at[which])

    c_send = copy(edge_first.at[layer, pl.ds(width, width), :], send_buf, 1)
    c_second = copy(edge_second.at[layer], second_buf, 2)
    c_node = copy(nodes, node_buf, 3)
    c_nf = copy(node_first.at[layer], nf_buf, 4)
    c_ns = copy(node_second.at[layer], ns_buf, 5)

    def c_before(b):
        return pltpu.make_async_copy(
            before.at[pl.ds(b * BLOCK, BLOCK), :], before_buf.at[pl.ds(b * BLOCK, BLOCK), :], bsem.at[0, b]
        )

    def c_edge(b):
        return pltpu.make_async_copy(
            edges.at[pl.ds(b * BLOCK, BLOCK), :], edge_buf.at[pl.ds(b * BLOCK, BLOCK), :], bsem.at[1, b]
        )

    def c_fresh(b):
        return pltpu.make_async_copy(
            fresh.at[pl.ds(b * BLOCK, BLOCK), :], fresh_out.at[pl.ds(b * BLOCK, BLOCK), :], out_sem.at[b]
        )

    c_send.start()
    c_second.start()
    for b in range(blocks):

        @pl.when(b < live_blocks)
        def _(b=b):
            c_before(b).start()
            if not last:
                c_edge(b).start()

    c_node.start()
    c_nf.start()
    c_ns.start()
    acc[...] = jnp.zeros_like(acc)
    fill_picker(oh_lists, lists, 0, oh_lists.shape[0], count, 0)
    c_send.wait()
    table[...] = dot(incoming[...], send_buf[...]).astype(bf16)
    c_second.wait()

    def advance(b, carry):
        fill_picker(oh, send, b * (BLOCK // 128), BLOCK, table.shape[0], count)
        c_before(b).wait()
        rows = pl.ds(pl.multiple_of(b * BLOCK, BLOCK), BLOCK)
        result = tail(dot(oh[...], table[...]) + before_buf[rows, :], second_buf[...])
        target = recv_rows[pl.ds(b, 1), :]
        scatter = jnp.where(
            lax.broadcasted_iota(jnp.int32, (count, BLOCK), 0) == jnp.broadcast_to(target, (count, BLOCK)), 1.0, 0.0
        ).astype(bf16)
        acc[...] += dot(scatter, result.astype(bf16))
        if not last:
            c_edge(b).wait()
            fresh[rows, :] = (edge_buf[rows, :].astype(f32) + result).astype(bf16)
            c_fresh(b).start()
        return carry

    lax.fori_loop(0, live_blocks, advance, 0)
    c_node.wait()
    c_nf.wait()
    c_ns.wait()
    now = node_buf[...]
    before_node = dot(now, nf_buf[:width, :]) + dot(acc[...].astype(bf16), nf_buf[width:, :])
    updated = (now.astype(f32) + tail(before_node, ns_buf[...])).astype(bf16)
    nodes_out[...] = updated
    picked = dot(oh_lists[...], updated)
    if last:
        half = width // 2
        place = lax.broadcasted_iota(jnp.int32, (picked.shape[0], half), 0) % 8
        picked = jnp.where(place < 4, picked[:, :half], picked[:, half:])
    outgoing[...] = picked.astype(bf16)
    if not last:

        def drain(b, carry):
            c_fresh(b).wait()
            return carry

        lax.fori_loop(0, live_blocks, drain, 0)


def run_layer(layer, last, live, send, recv_rows, lists, incoming, before, edges, nodes, ef, es, nf, ns):
    count, width = nodes.shape
    edge_count = edges.shape[0]
    blocks = edge_count // BLOCK
    out_rows = lists.shape[0] * 128
    vm = pl.BlockSpec(memory_space=VMEM)
    hb = pl.BlockSpec(memory_space=HBM)
    out_shape = [
        jax.ShapeDtypeStruct((count, width), bf16),
        jax.ShapeDtypeStruct((out_rows, width // 2 if last else width), bf16),
    ]
    out_specs = [vm, vm]
    scratch = []
    if not last:
        out_shape.append(jax.ShapeDtypeStruct((edge_count, width), bf16))
        out_specs.append(hb)
        scratch += [VMEM((edge_count, width), bf16), VMEM((edge_count, width), bf16), pltpu.SemaphoreType.DMA((blocks,))]
    scratch += [
        VMEM((width, width), bf16),
        VMEM((edge_count, width), f32),
        VMEM((width, width), bf16),
        VMEM((count, width), bf16),
        VMEM((2 * width, width), bf16),
        VMEM((width, width), bf16),
        VMEM(incoming.shape, bf16),
        VMEM((BLOCK, incoming.shape[0]), bf16),
        VMEM((out_rows, count), bf16),
        VMEM((count, width), f32),
        pltpu.SemaphoreType.DMA((6,)),
        pltpu.SemaphoreType.DMA((2, blocks)),
    ]
    return pl.pallas_call(
        functools.partial(layer_kernel, layer, last),
        out_shape=out_shape,
        in_specs=[pl.BlockSpec(memory_space=pltpu.SMEM), vm, vm, vm, vm] + [hb] * 7,
        out_specs=out_specs,
        scratch_shapes=scratch,
        compiler_params=pltpu.CompilerParams(vmem_limit_bytes=GRANT),
        cost_estimate=pl.CostEstimate(flops=9 * edge_count * width * width, bytes_accessed=12 << 20, transcendentals=0),
        name=f"layer_{layer}",
    )(live, send, recv_rows, lists, incoming, before, edges, nodes, ef, es, nf, ns)


def decode_before_kernel(edges, grid, first, grid_first, out, out_grid):
    width = grid.shape[1]
    cells = grid.shape[0]
    out_grid[...] = dot(grid[...], grid_first[...])
    rows = edges[...].reshape(3 * cells, width)
    own = dot(rows, first[:width, :]).reshape(3, cells, width)
    out[...] = own + dot(grid[...], first[2 * width :, :])[None]


def decode_before(edges, grid, first, grid_first):
    cells, width = grid.shape
    whole = lambda i: (0, 0)
    return pl.pallas_call(
        decode_before_kernel,
        grid=(cells // CELLS,),
        in_specs=[
            pl.BlockSpec((3, CELLS, width), lambda i: (0, i, 0)),
            pl.BlockSpec((CELLS, width), lambda i: (i, 0)),
            pl.BlockSpec((3 * width, width), whole),
            pl.BlockSpec((width, width), whole),
        ],
        out_specs=[
            pl.BlockSpec((3, CELLS, width), lambda i: (0, i, 0)),
            pl.BlockSpec((CELLS, width), lambda i: (i, 0)),
        ],
        out_shape=[
            jax.ShapeDtypeStruct((3, cells, width), f32),
            jax.ShapeDtypeStruct((cells, width), f32),
        ],
        compiler_params=pltpu.CompilerParams(vmem_limit_bytes=GRANT),
        cost_estimate=pl.CostEstimate(flops=10 * cells * width * width, bytes_accessed=14 << 20, transcendentals=0),
        name="decode_before",
    )(edges, grid, first, grid_first)


def decode_kernel(
    sources, incoming, before, before_grid, grid, first, second, grid_first, grid_second, out,
    mid_buf, before_buf, bg_buf, grid_buf, second_buf, gf_buf, gs_buf, table, oh, out_buf, sem, bsem, osem,
):
    width = grid.shape[1]
    cells = grid.shape[0]
    blocks = cells // CELLS
    half = width // 2

    def copy(src, dst, which):
        return pltpu.make_async_copy(src, dst, sem.at[which])

    c_mid = copy(first.at[pl.ds(width, width), :], mid_buf, 1)
    c_second = copy(second, second_buf, 2)
    c_gf = copy(grid_first.at[pl.ds(width, width), :], gf_buf, 3)
    c_gs = copy(grid_second, gs_buf, 4)

    def c_before(b):
        rows = pl.ds(b * CELLS, CELLS)
        return pltpu.make_async_copy(before.at[:, rows, :], before_buf.at[:, rows, :], bsem.at[0, b])

    def c_bg(b):
        rows = pl.ds(b * CELLS, CELLS)
        return pltpu.make_async_copy(before_grid.at[rows, :], bg_buf.at[rows, :], bsem.at[1, b])

    def c_grid(b):
        rows = pl.ds(b * CELLS, CELLS)
        return pltpu.make_async_copy(grid.at[rows, :], grid_buf.at[rows, :], bsem.at[2, b])

    def c_out(b):
        rows = pl.ds(b * CELLS, CELLS)
        return pltpu.make_async_copy(out_buf.at[rows, :], out.at[rows, :], osem.at[b])

    c_mid.start()
    c_before(0).start()
    c_second.start()
    c_gf.start()
    c_gs.start()
    c_bg(0).start()
    c_grid(0).start()
    for b in range(1, blocks):
        c_before(b).start()
        c_bg(b).start()
        c_grid(b).start()
    packed = incoming[...].astype(f32).reshape(cells // 16, 16, half)
    even, odd = packed[:, :8, :], packed[:, 8:, :]
    low = lax.broadcasted_iota(jnp.int32, even.shape, 1) < 4
    left = jnp.where(low, even, pltpu.roll(odd, 4, 1))
    right = jnp.where(low, pltpu.roll(even, 4, 1), odd)
    left = left.reshape(cells // 2, half).astype(bf16)
    right = right.reshape(cells // 2, half).astype(bf16)
    c_mid.wait()
    table[...] = (dot(left, mid_buf[:half, :]) + dot(right, mid_buf[half:, :])).astype(bf16)
    c_second.wait()
    c_gf.wait()
    c_gs.wait()
    steps = CELLS // 128

    def advance(b, carry):
        rows = pl.ds(pl.multiple_of(b * CELLS, CELLS), CELLS)
        c_before(b).wait()
        summed = jnp.zeros((CELLS, width), f32)
        for branch in range(3):
            fill_picker(oh.at[branch], sources, branch * (cells // 128) + b * steps, CELLS, table.shape[0], 0)
            result = tail(dot(oh[branch], table[...]) + before_buf[branch, rows, :], second_buf[...])
            summed = summed + result.astype(bf16).astype(f32)
        c_bg(b).wait()
        c_grid(b).wait()
        result = tail(dot(summed.astype(bf16), gf_buf[...]) + bg_buf[rows, :], gs_buf[...])
        out_buf[rows, :] = (grid_buf[rows, :].astype(f32) + result).astype(bf16)
        c_out(b).start()
        return carry

    lax.fori_loop(0, blocks, advance, 0)

    def drain(b, carry):
        c_out(b).wait()
        return carry

    lax.fori_loop(0, blocks, drain, 0)


def decode(sources, incoming, before, before_grid, grid, first, second, grid_first, grid_second):
    cells, width = grid.shape
    blocks = cells // CELLS
    hb = pl.BlockSpec(memory_space=HBM)
    return pl.pallas_call(
        decode_kernel,
        out_shape=jax.ShapeDtypeStruct((cells, width), bf16),
        in_specs=[pl.BlockSpec(memory_space=VMEM)] * 2 + [hb] * 7,
        out_specs=hb,
        scratch_shapes=[
            VMEM((width, width), bf16),
            VMEM((3, cells, width), f32),
            VMEM((cells, width), f32),
            VMEM((cells, width), bf16),
            VMEM((width, width), bf16),
            VMEM((width, width), bf16),
            VMEM((width, width), bf16),
            VMEM((incoming.shape[0] // 2, width), bf16),
            VMEM((3, CELLS, incoming.shape[0] // 2), bf16),
            VMEM((cells, width), bf16),
            pltpu.SemaphoreType.DMA((5,)),
            pltpu.SemaphoreType.DMA((3, blocks)),
            pltpu.SemaphoreType.DMA((blocks,)),
        ],
        compiler_params=pltpu.CompilerParams(vmem_limit_bytes=GRANT),
        cost_estimate=pl.CostEstimate(flops=16 * cells * width * width, bytes_accessed=13 << 20, transcendentals=0),
        name="decode",
    )(sources, incoming, before, before_grid, grid, first, second, grid_first, grid_second)


def exchange(rows):
    chunks = rows.reshape(-1, 8, rows.shape[1])
    return lax.all_to_all(chunks, ("lat", "lon"), split_axis=0, concat_axis=0, tiled=True).reshape(rows.shape)


def shards(
    mesh_nodes,
    mesh_edges,
    grid_state,
    decoder_edges,
    edge_send,
    edge_recv,
    halo_lists,
    decoder_lists,
    decoder_sources,
    edge_first,
    edge_second,
    node_first,
    node_second,
    decoder_first,
    decoder_second,
    grid_first,
    grid_second,
):
    tile_lat, tile_lon, width = grid_state.shape
    cells = tile_lat * tile_lon
    halo = halo_lists.reshape(-1, 128)
    outgoing = pick_first(halo, mesh_nodes)
    incoming = exchange(outgoing)
    live = (jnp.sum((edge_recv >= 0).astype(jnp.int32)) + (BLOCK - 1)) // BLOCK
    live = live.reshape(1)
    send = edge_send.reshape(-1, 128)
    recv = edge_recv.reshape(-1, 128)
    recv_rows = edge_recv.reshape(-1, BLOCK)
    decoder_rows = decoder_lists.reshape(decoder_lists.shape[1], decoder_lists.shape[2])
    decoder_rows = jnp.concatenate([decoder_rows, decoder_rows], axis=1).reshape(-1, 128)
    grid = grid_state.reshape(cells, width)
    sources = decoder_sources.reshape(-1, 128)
    nodes, edges = mesh_nodes, mesh_edges
    layers = edge_first.shape[0]
    for layer in range(layers):
        last = layer == layers - 1
        before = edges_before(live, edges, send, recv, nodes, edge_first, layer)
        results = run_layer(
            layer, last, live, send, recv_rows, decoder_rows if last else halo, incoming, before, edges, nodes,
            edge_first, edge_second, node_first, node_second,
        )
        nodes, outgoing = results[:2]
        if not last:
            edges = results[2]
        incoming = exchange(outgoing)
    before, before_grid = decode_before(decoder_edges.reshape(3, cells, width), grid, decoder_first, grid_first)
    final = decode(
        sources, incoming, before, before_grid, grid, decoder_first, decoder_second, grid_first, grid_second
    )
    return nodes, final.reshape(tile_lat, tile_lon, width)


def solution(mesh):
    placed = (
        P(("lat", "lon"), None),
        P(("lat", "lon"), None),
        P("lat", "lon", None),
        P(None, "lat", "lon", None),
        P(("lat", "lon")),
        P(("lat", "lon")),
        P(("lat", "lon"), None, None),
        P(("lat", "lon"), None, None),
        P(None, "lat", "lon"),
        P(),
        P(),
        P(),
        P(),
        P(),
        P(),
        P(),
        P(),
    )
    return jax.shard_map(
        shards,
        mesh=mesh,
        in_specs=placed,
        out_specs=(P(("lat", "lon"), None), P("lat", "lon", None)),
        check_vma=False,
    )
```

time: 257 us -> 121 us (0.47); the launches traced: 254 us -> 121 us
  matrix products: 68.9 us -> 0 us
  Pallas kernels: 0 us -> 49 us
  starting transfers between devices: 76.3 us -> 31.5 us
  local copies, waits for them, and re-layouts: 42.6 us -> 6.3 us
  other arithmetic: 27.3 us -> 0.66 us
  waiting for transfers between devices: 37.1 us -> 32.4 us
    dot_general x27 -> x0, matrix products: 68.9 us -> none  [the longest x12 45.9 us: perceptron(): jnp.dot(hidden, layer_two, preferred_element_type=jnp.float32)]
    pallas_call x0 -> x7, Pallas kernels: none -> 49 us  [the longest x1 15.6 us: decode(): pl.pallas_call(decode_kernel, out_shape=jax.ShapeDtypeStruct((cells, widt...]
    all_to_all x3, starting transfers between devices: 76.3 us -> 31.5 us  [exchange(): lax.all_to_all(chunks, ('lat', 'lon'), split_axis=0, concat_axis=0, tiled...]
    dynamic_slice x20 -> x0, local copies, waits for them, and re-layouts: 14.7 us -> none  [the longest x4 7.85 us: decode_advance(): grid_block = lax.dynamic_slice_in_dim(flat_grid, first_row, block_rows, 0)]
    reduce_sum x13 -> x1, other arithmetic: 13.3 us -> 0.66 us  [shards(): live = (jnp.sum((edge_recv >= 0).astype(jnp.int32)) + (BLOCK - 1)) // BLOCK]
    convert_element_type x14 -> x0, other arithmetic: 10.5 us -> none  [the longest x2 4.07 us: decode_advance(): fresh = (grid_block.astype(jnp.float32) + result).astype(jnp.bfloat16)]
    dynamic_update_slice x4 -> x0, local copies, waits for them, and re-layouts: 7.82 us -> none  [decode_advance(): return lax.dynamic_update_slice_in_dim(updated, fresh, first_row, 0)]
    while x40 -> x0, local copies, waits for them, and re-layouts: 6.22 us -> none  [the longest x1 3.19 us: decode(): decoded = lax.fori_loop(0, cells // block_rows, decode_advance, flat_grid)]
  transfers between devices with their start and end apart: 3 -> 3, of which waited for: 3 -> 3; matrix products, arithmetic and copies ran while one was open for 5% -> 2% of each run, Pallas kernels for 0% -> 13%
where the time goes in v1:
time: 121 us
  Pallas kernels  49 us (40%)
  waiting for transfers between devices  32.4 us (27%)
  starting transfers between devices  31.5 us (26%)
  local copies, waits for them, and re-layouts  6.3 us (5%)
  between operations  1.52 us (1%)
    all_to_all x3, waiting for transfers between devices, exchange(): lax.all_to_all(chunks, ('lat', 'lon'), split_axis=0, concat_axis=0, tiled...  32.4 us
    all_to_all x3, starting transfers between devices, exchange(): lax.all_to_all(chunks, ('lat', 'lon'), split_axis=0, concat_axis=0, tiled...  31.5 us
    pallas_call x1, Pallas kernels, decode(): pl.pallas_call(decode_kernel, out_shape=jax.ShapeDtypeStruct((cells, widt...  15.6 us
    pallas_call x2, Pallas kernels, run_layer(): pl.pallas_call(functools.partial(layer_kernel, layer, last), out_shape=ou...  14.7 us
    pallas_call x2, Pallas kernels, edges_before(): pl.pallas_call(before_kernel, grid_spec=grid_spec, out_shape=jax.ShapeDty...  8.24 us
    pallas_call x1, Pallas kernels, decode_before(): pl.pallas_call(decode_before_kernel, grid=(cells // CELLS,), in_specs=[pl...  8.03 us
    unnamed x13, local copies, waits for them, and re-layouts  3.57 us
    pallas_call x1, Pallas kernels, pick_first(): pl.pallas_call(pick_kernel, out_shape=jax.ShapeDtypeStruct((rows, nodes.s...  2.42 us
  transfers between devices with their start and end apart: 3, of which 3 were waited for; matrix products, arithmetic and copies ran while one was open for 2% of the time, Pallas kernels for 13%

profile of v1, /device:TPU:1, one launch (start us, length us, event | category | flops | bytes accessed | tf_op | source)
XLA Modules:
  0.0 121.4 jit_solution(8139734485791938279)
XLA Ops:
  0.6 0.0 copy-start.4
  0.6 0.8 copy.22
  1.4 0.7 reshape.60.lists
  2.1 2.4 %pick_first.1 = bf16[1024,512]{1,0:T(8,128)(2,1)} custom-call(s32[8,128]{1,0:T(8,128)} %reshape.60.lists, bf16[256,512]{1,0:T(8,128)(2,1)} %nodes.5), custom_call_target="tpu_custom_call" | custom-call | flops 268435456 | bytes 1048576 | tf_op jit(solution)/shard_map/pick_first/pallas_call | solution.py:64
  4.5 11.5 %all-to-all-start = ((bf16[128,8,512]{2,1,0:T(8,128)(2,1)}), bf16[128,8,512]{2,1,0:T(8,128)(2,1)S(1)}, u32[]{:S(2)}, u32[]{:S(2)}) async-start(bf16[128,8,512]{2,1,0:T(8,128)(2,1)} %bitcast.13), calls=%async_computation | async-start | bytes 2097152 | tf_op jit(solution)/shard_map/all_to_all | solution.py:429
  16.0 0.0 copy-done.4
  16.0 0.7 convert_reduce_fusion
  17.3 0.6 reshape.57.recv_rows
  17.9 4.1 %edges_before_0.1.before = f32[2048,512]{1,0:T(8,128)} custom-call(s32[1]{0:T(128)} %bitcast.live, bf16[2048,512]{1,0:T(8,128)(2,1)} %edges.3, s32[16,128]{1,0:T(8,128)} %bitcast.25, s32[16,128]{1,0:T(8,128)} %bitcast.19, bf16[256,512]{1,0:T(8,128)(2,1)} %nodes.5, bf16[2,1536,512]{2,1,0:T(8,128)(2,1)} %edge_first.3), custom_call_target="tpu_custom_call" | custom-call | flops 4294967296 | bytes 8388608 | tf_op jit(solution)/shard_map/edges_before_0/pallas_call | solution.py:113
  22.1 12.9 %all-to-all-done = bf16[128,8,512]{2,1,0:T(8,128)(2,1)S(1)} async-done(((bf16[128,8,512]{2,1,0:T(8,128)(2,1)}), bf16[128,8,512]{2,1,0:T(8,128)(2,1)S(1)}, u32[]{:S(2)}, u32[]{:S(2)}) %all-to-all-start) | async-done | bytes 1048608 | tf_op jit(solution)/shard_map/all_to_all | solution.py:429
  34.9 0.0 copy-start
  34.9 1.0 copy-done
  35.9 0.0 copy-start.5
  35.9 7.8 %layer_0.1 = (bf16[256,512]{1,0:T(8,128)(2,1)}, bf16[1024,512]{1,0:T(8,128)(2,1)}, bf16[2048,512]{1,0:T(8,128)(2,1)}) custom-call(s32[1]{0:T(128)} %bitcast.live, s32[16,128]{1,0:T(8,128)} %bitcast.26, s32[4,512]{1,0:T(4,128)} %reshape.57.recv_rows, s32[8,128]{1,0:T(8,128)} %reshape.60.lists, bf16[1024,512]{1,0:T(8,128)(2,1)} %bitcast.14, ...), custom_call_target="tpu_custom_call" | custom-call | flops 4831838208 | bytes 12582912 | tf_op jit(solution)/shard_map/layer_0/pallas_call | solution.py:268
  43.7 10.3 %all-to-all-start.1 = ((bf16[128,8,512]{2,1,0:T(8,128)(2,1)}), bf16[128,8,512]{2,1,0:T(8,128)(2,1)S(1)}, u32[]{:S(2)}, u32[]{:S(2)}) async-start(bf16[128,8,512]{2,1,0:T(8,128)(2,1)} %bitcast.16), calls=%async_computation.1 | async-start | bytes 2097152 | tf_op jit(solution)/shard_map/all_to_all | solution.py:429
  54.0 0.0 copy-done.5
  54.0 0.1 copy.21
  54.1 0.7 reshape.59.lists
  54.8 4.1 %edges_before_1.1.before = f32[2048,512]{1,0:T(8,128)} custom-call(s32[1]{0:T(128)} %bitcast.live, bf16[2048,512]{1,0:T(8,128)(2,1)} %get-tuple-element.10.edges, s32[16,128]{1,0:T(8,128)} %bitcast.27, s32[16,128]{1,0:T(8,128)} %bitcast.20, bf16[256,512]{1,0:T(8,128)(2,1)} %get-tuple-element.11.nodes, bf16[2,1536,512]{2,1,0:T(8,128)(2,1)} %edge_first.3), custom_call_target="tpu_custom_call" | custom-call | flops 4294967296 | bytes 8388608 | tf_op jit(solution)/shard_map/edges_before_1/pallas_call | solution.py:113
  58.9 14.1 %all-to-all-done.1 = bf16[128,8,512]{2,1,0:T(8,128)(2,1)S(1)} async-done(((bf16[128,8,512]{2,1,0:T(8,128)(2,1)}), bf16[128,8,512]{2,1,0:T(8,128)(2,1)S(1)}, u32[]{:S(2)}, u32[]{:S(2)}) %all-to-all-start.1) | async-done | bytes 1048608 | tf_op jit(solution)/shard_map/all_to_all | solution.py:429
  73.0 0.0 copy-start.1
  73.0 1.0 copy-done.1
  74.0 0.0 copy-start.3
  74.0 6.9 %layer_1.1 = (bf16[256,512]{1,0:T(8,128)(2,1)}, bf16[1024,256]{1,0:T(8,128)(2,1)}) custom-call(s32[1]{0:T(128)} %bitcast.live, s32[16,128]{1,0:T(8,128)} %bitcast.28, s32[4,512]{1,0:T(4,128)} %reshape.57.recv_rows, s32[8,128]{1,0:T(8,128)} %reshape.59.lists, bf16[1024,512]{1,0:T(8,128)(2,1)} %bitcast.15, f32[2048,512]{1,0:T(8,128)} %edges_before_1.1.before, ...), custom_call_target="tpu_custom_call" | custom-call | flops 4831838208 | bytes 12582912 | tf_op jit(solution)/shard_map/layer_1/pallas_call | solution.py:268
  80.9 9.7 %all-to-all-start.2 = ((bf16[128,8,256]{2,1,0:T(8,128)(2,1)}), bf16[128,8,256]{2,1,0:T(8,128)(2,1)S(1)}, u32[]{:S(2)}, u32[]{:S(2)}) async-start(bf16[128,8,256]{2,1,0:T(8,128)(2,1)} %bitcast.17), calls=%async_computation.2 | async-start | bytes 1048576 | tf_op jit(solution)/shard_map/all_to_all | solution.py:429
  90.6 0.0 copy-done.3
  90.6 0.7 reshape.66.sources
  91.3 8.0 %decode_before.1 = (f32[3,1024,512]{2,1,0:T(8,128)}, f32[1024,512]{1,0:T(8,128)}) custom-call(bf16[3,1024,512]{2,1,0:T(8,128)(2,1)} %bitcast.22, bf16[1024,512]{1,0:T(8,128)(2,1)} %bitcast.23, bf16[1536,512]{1,0:T(8,128)(2,1)} %first.7, bf16[1024,512]{1,0:T(8,128)(2,1)} %grid_first.3), custom_call_target="tpu_custom_call" | custom-call | flops 2684354560 | bytes 14680064 | tf_op jit(solution)/shard_map/decode_before/pallas_call | solution.py:292
  99.3 5.5 %all-to-all-done.2 = bf16[128,8,256]{2,1,0:T(8,128)(2,1)S(1)} async-done(((bf16[128,8,256]{2,1,0:T(8,128)(2,1)}), bf16[128,8,256]{2,1,0:T(8,128)(2,1)S(1)}, u32[]{:S(2)}, u32[]{:S(2)}) %all-to-all-start.2) | async-done | bytes 524320 | tf_op jit(solution)/shard_map/all_to_all | solution.py:429
  104.8 0.0 copy-start.2
  104.8 0.8 copy-done.2
  105.6 15.6 %decode.1 = bf16[1024,512]{1,0:T(8,128)(2,1)} custom-call(s32[24,128]{1,0:T(8,128)} %reshape.66.sources, bf16[1024,256]{1,0:T(8,128)(2,1)} %bitcast.18, f32[3,1024,512]{2,1,0:T(8,128)} %get-tuple-element.14.before, f32[1024,512]{1,0:T(8,128)} %get-tuple-element.15.before_grid, bf16[1024,512]{1,0:T(8,128)(2,1)} %bitcast.24, bf16[1536,512]{1,0:T(8,128)(2,1)} %first.7, ...), custom_call_target="tpu_custom_call" | custom-call | flops 4294967296 | bytes 13631488 | tf_op jit(solution)/shard_map/decode/pallas_call | solution.py:401
  (1 shorter events, 0.0 us)
Async XLA Ops:
  0.6 15.4 %copy-start.4 = (s32[2048]{0:T(1024)S(1)}, s32[2048]{0:T(1024)}, u32[]{:S(2)}) copy-start(s32[2048]{0:T(1024)} %param.22) | copy-start | bytes 24580
  4.5 30.4 %all-to-all-start = ((bf16[128,8,512]{2,1,0:T(8,128)(2,1)}), bf16[128,8,512]{2,1,0:T(8,128)(2,1)S(1)}, u32[]{:S(2)}, u32[]{:S(2)}) async-start(bf16[128,8,512]{2,1,0:T(8,128)(2,1)} %bitcast.13), calls=%async_computation | async-start | bytes 2097152 | tf_op jit(solution)/shard_map/all_to_all | solution.py:429
  34.9 1.0 copy-start
  35.9 18.1 %copy-start.5 = (s32[1,128,4]{1,2,0:T(4,128)S(1)}, s32[1,128,4]{1,2,0:T(4,128)}, u32[]{:S(2)}) copy-start(s32[1,128,4]{1,2,0:T(4,128)} %param.24) | copy-start | bytes 6148
  43.7 29.3 %all-to-all-start.1 = ((bf16[128,8,512]{2,1,0:T(8,128)(2,1)}), bf16[128,8,512]{2,1,0:T(8,128)(2,1)S(1)}, u32[]{:S(2)}, u32[]{:S(2)}) async-start(bf16[128,8,512]{2,1,0:T(8,128)(2,1)} %bitcast.16), calls=%async_computation.1 | async-start | bytes 2097152 | tf_op jit(solution)/shard_map/all_to_all | solution.py:429
  73.0 1.0 copy-start.1
  74.0 16.6 %copy-start.3 = (s32[3,32,32]{2,1,0:T(8,128)S(1)}, s32[3,32,32]{2,1,0:T(8,128)}, u32[]{:S(2)}) copy-start(s32[3,32,32]{2,1,0:T(8,128)} %param.25) | copy-start | bytes 36868
  80.9 23.9 %all-to-all-start.2 = ((bf16[128,8,256]{2,1,0:T(8,128)(2,1)}), bf16[128,8,256]{2,1,0:T(8,128)(2,1)S(1)}, u32[]{:S(2)}, u32[]{:S(2)}) async-start(bf16[128,8,256]{2,1,0:T(8,128)(2,1)} %bitcast.17), calls=%async_computation.2 | async-start | bytes 1048576 | tf_op jit(solution)/shard_map/all_to_all | solution.py:429
  104.8 0.8 copy-start.2

commit v2 on v1

--- a/solution.py
+++ b/solution.py
@@ -9,20 +9,25 @@
 
 epsilon = 1e-05
 BLOCK = 512
+SUB = 256
+CHUNK = 32
 CELLS = 256
-GRANT = 62 << 20
+GRANT = 40 << 20
 bf16 = jnp.bfloat16
 f32 = jnp.float32
 HBM = pltpu.HBM
 VMEM = pltpu.VMEM
 
 
+def pinned(*arrays):
+    return [pltpu.with_memory_space_constraint(a, HBM) for a in arrays]
+
+
 def dot(a, b):
     return jnp.dot(a, b, preferred_element_type=f32)
 
 
-def silu(values):
-    half = values * 0.5
+def silu_of_double(half):
     return half + half * jnp.tanh(half)
 
 
@@ -33,8 +38,8 @@
     return centered * lax.rsqrt(spread + epsilon)
 
 
-def tail(before, second):
-    return normalize(dot(silu(before).astype(bf16), second))
+def tail(half, second):
+    return normalize(dot(silu_of_double(half).astype(bf16), second))
 
 
 def picker_rows(row, table_rows, first):
@@ -54,19 +59,30 @@
         oh_ref[r * 128 : (r + 1) * 128, :] = picker_rows(row, table_rows, first)
 
 
-def pick_kernel(lists, nodes, out, oh):
-    fill_picker(oh, lists, 0, out.shape[0], nodes.shape[0], 0)
+def fill_lists(oh_ref, lists_ref, spread_ref):
+    slots = lists_ref.shape[0]
+    for s in range(8):
+        row = lists_ref[s % slots : s % slots + 1, :]
+        spread_ref[pl.ds(s, 128, stride=8), :] = jnp.broadcast_to(row.astype(f32), (128, 128)).T
+    lanes = lax.broadcasted_iota(jnp.int32, spread_ref.shape, 1).astype(f32)
+    shifted = spread_ref[...] - lanes
+    for c in range(oh_ref.shape[1] // 128):
+        oh_ref[:, c * 128 : (c + 1) * 128] = jnp.where(shifted == float(c * 128), 1.0, 0.0).astype(bf16)
+
+
+def pick_kernel(lists, nodes, out, oh, spread):
+    fill_lists(oh, lists, spread)
     out[...] = dot(oh[...], nodes[...]).astype(bf16)
 
 
 def pick_first(lists, nodes):
-    rows = lists.shape[0] * 128
+    rows = lists.shape[1] * 8
     return pl.pallas_call(
         pick_kernel,
         out_shape=jax.ShapeDtypeStruct((rows, nodes.shape[1]), bf16),
         in_specs=[pl.BlockSpec(memory_space=VMEM)] * 2,
         out_specs=pl.BlockSpec(memory_space=VMEM),
-        scratch_shapes=[VMEM((rows, nodes.shape[0]), bf16)],
+        scratch_shapes=[VMEM((rows, nodes.shape[0]), bf16), VMEM((rows, 128), f32)],
         compiler_params=pltpu.CompilerParams(vmem_limit_bytes=GRANT),
         cost_estimate=pl.CostEstimate(
             flops=2 * rows * nodes.shape[0] * nodes.shape[1], bytes_accessed=1 << 20, transcendentals=0
@@ -75,37 +91,34 @@
     )(lists, nodes)
 
 
-def before_kernel(live, edges, send, recv, nodes, first, out, oh):
+def before_kernel(edges, send, recv, nodes, first, out, oh):
     block = pl.program_id(0)
     width = nodes.shape[1]
     count = nodes.shape[0]
 
-    @pl.when(block < live[0])
-    def _():
-        rows = edges.shape[0]
-        steps = rows // 128
-        fill_picker(oh, send, block * steps, rows, count, 0)
-        from_send = dot(oh[...], nodes[...]).astype(bf16)
-        total = dot(edges[...], first[0, :width, :]) + dot(from_send, first[0, width : 2 * width, :])
-        fill_picker(oh, recv, block * steps, rows, count, 0)
-        from_recv = dot(oh[...], nodes[...]).astype(bf16)
-        out[...] = total + dot(from_recv, first[0, 2 * width :, :])
-
-
-def edges_before(live, edges, send, recv, nodes, edge_first, layer):
+    rows = edges.shape[0]
+    steps = rows // 128
+    fill_picker(oh, send, block * steps, rows, count, 0)
+    from_send = dot(oh[...], nodes[...]).astype(bf16)
+    total = dot(edges[...], first[0, :width, :]) + dot(from_send, first[0, width : 2 * width, :])
+    fill_picker(oh, recv, block * steps, rows, count, 0)
+    from_recv = dot(oh[...], nodes[...]).astype(bf16)
+    out[...] = (0.5 * (total + dot(from_recv, first[0, 2 * width :, :]))).astype(bf16)
+
+
+def edges_before(edges, send, recv, nodes, edge_first, layer):
     count, width = edges.shape
     blocks = count // BLOCK
-    clamp = lambda i, live: (jnp.minimum(i, live[0] - 1), 0)
-    whole = lambda i, live: (0, 0)
-    grid_spec = pltpu.PrefetchScalarGridSpec(
-        num_scalar_prefetch=1,
+    clamp = lambda i: (i, 0)
+    whole = lambda i: (0, 0)
+    grid_spec = pl.GridSpec(
         grid=(blocks,),
         in_specs=[
             pl.BlockSpec((BLOCK, width), clamp),
             pl.BlockSpec(send.shape, whole),
             pl.BlockSpec(recv.shape, whole),
             pl.BlockSpec(nodes.shape, whole),
-            pl.BlockSpec((1, 3 * width, width), lambda i, live: (layer, 0, 0)),
+            pl.BlockSpec((1, 3 * width, width), lambda i: (layer, 0, 0)),
         ],
         out_specs=pl.BlockSpec((BLOCK, width), clamp),
         scratch_shapes=[VMEM((BLOCK, nodes.shape[0]), bf16)],
@@ -113,19 +126,18 @@
     return pl.pallas_call(
         before_kernel,
         grid_spec=grid_spec,
-        out_shape=jax.ShapeDtypeStruct((count, width), f32),
+        out_shape=jax.ShapeDtypeStruct((count, width), bf16),
         compiler_params=pltpu.CompilerParams(vmem_limit_bytes=GRANT),
         cost_estimate=pl.CostEstimate(flops=8 * count * width * width, bytes_accessed=8 << 20, transcendentals=0),
         name=f"edges_before_{layer}",
-    )(live, edges, send, recv, nodes, edge_first)
+    )(edges, send, recv, nodes, edge_first)
 
 
 def layer_kernel(
     layer,
     last,
-    live,
     send,
-    recv_rows,
+    recv,
     lists,
     incoming,
     before,
@@ -146,11 +158,10 @@
         rest = rest[3:]
         edge_buf, fresh, out_sem = rest[:3]
         rest = rest[3:]
-    send_buf, before_buf, second_buf, node_buf, nf_buf, ns_buf, table, oh, oh_lists, acc, sem, bsem = rest
+    send_buf, before_buf, second_buf, node_buf, nf_buf, ns_buf, table, oh, ready, oh_lists, acc, spread, hidden, raw, message, scatter, sem, bsem = rest
     width = nodes.shape[1]
     count = nodes.shape[0]
     blocks = before.shape[0] // BLOCK
-    live_blocks = live[0]
 
     def copy(src, dst, which):
         return pltpu.make_async_copy(src, dst, sem.at[which])
@@ -177,46 +188,79 @@
         )
 
     c_send.start()
+    c_before(0).start()
     c_second.start()
-    for b in range(blocks):
-
-        @pl.when(b < live_blocks)
-        def _(b=b):
-            c_before(b).start()
-            if not last:
-                c_edge(b).start()
-
+    for b in range(1, blocks):
+        c_before(b).start()
+    if not last:
+        for b in range(blocks):
+            c_edge(b).start()
     c_node.start()
     c_nf.start()
     c_ns.start()
-    acc[...] = jnp.zeros_like(acc)
-    fill_picker(oh_lists, lists, 0, oh_lists.shape[0], count, 0)
+    steps = SUB // 128
+    items = before.shape[0] // SUB
+
+    def picker(i):
+        fill_picker(oh.at[i % 3], send, i * steps, SUB, table.shape[0], count)
+
+    def first_half(i, part):
+        columns = slice(part * (width // 2), (part + 1) * (width // 2))
+        ready[i % 2, :, columns] = dot(oh[i % 3], table[:, columns])
+
+    def hide(i):
+        for c in range(0, SUB, CHUNK):
+            half = ready[i % 2, c : c + CHUNK, :] + before_buf[i * SUB + c : i * SUB + c + CHUNK, :].astype(f32)
+            hidden[c : c + CHUNK, :] = silu_of_double(half).astype(bf16)
+
+    def finish(i):
+        for r in range(steps):
+            row = jnp.broadcast_to(recv[i * steps + r : i * steps + r + 1, :], (count, 128))
+            hit = lax.broadcasted_iota(jnp.int32, (count, 128), 0) == row
+            scatter[:, r * 128 : (r + 1) * 128] = jnp.where(hit, 1.0, 0.0).astype(bf16)
+        for c in range(0, SUB, CHUNK):
+            rows = slice(i * SUB + c, i * SUB + c + CHUNK)
+            result = normalize(raw[c : c + CHUNK, :])
+            message[c : c + CHUNK, :] = result.astype(bf16)
+            if not last:
+                fresh[rows, :] = (edge_buf[rows, :].astype(f32) + result).astype(bf16)
+        part = dot(scatter[...], message[...])
+        if i == 0:
+            acc[...] = part
+        else:
+            acc[...] += part
+
+    picker(0)
+    picker(1)
+    fill_lists(oh_lists, lists, spread)
     c_send.wait()
-    table[...] = dot(incoming[...], send_buf[...]).astype(bf16)
+    table[...] = (0.5 * dot(incoming[...], send_buf[...])).astype(bf16)
     c_second.wait()
-
-    def advance(b, carry):
-        fill_picker(oh, send, b * (BLOCK // 128), BLOCK, table.shape[0], count)
-        c_before(b).wait()
-        rows = pl.ds(pl.multiple_of(b * BLOCK, BLOCK), BLOCK)
-        result = tail(dot(oh[...], table[...]) + before_buf[rows, :], second_buf[...])
-        target = recv_rows[pl.ds(b, 1), :]
-        scatter = jnp.where(
-            lax.broadcasted_iota(jnp.int32, (count, BLOCK), 0) == jnp.broadcast_to(target, (count, BLOCK)), 1.0, 0.0
-        ).astype(bf16)
-        acc[...] += dot(scatter, result.astype(bf16))
-        if not last:
-            c_edge(b).wait()
-            fresh[rows, :] = (edge_buf[rows, :].astype(f32) + result).astype(bf16)
-            c_fresh(b).start()
-        return carry
-
-    lax.fori_loop(0, live_blocks, advance, 0)
+    per = BLOCK // SUB
+    c_before(0).wait()
+    first_half(0, 0)
+    first_half(0, 1)
+    for i in range(items):
+        if i + 1 < items and (i + 1) % per == 0:
+            c_before((i + 1) // per).wait()
+        if not last and i % per == 0:
+            c_edge(i // per).wait()
+        if i + 2 < items:
+            picker(i + 2)
+        hide(i)
+        if i + 1 < items:
+            first_half(i + 1, 0)
+        raw[...] = dot(hidden[...], second_buf[...])
+        if i + 1 < items:
+            first_half(i + 1, 1)
+        finish(i)
+        if not last and (i + 1) % (BLOCK // SUB) == 0:
+            c_fresh(i // (BLOCK // SUB)).start()
     c_node.wait()
     c_nf.wait()
     c_ns.wait()
     now = node_buf[...]
-    before_node = dot(now, nf_buf[:width, :]) + dot(acc[...].astype(bf16), nf_buf[width:, :])
+    before_node = 0.5 * (dot(now, nf_buf[:width, :]) + dot(acc[...].astype(bf16), nf_buf[width:, :]))
     updated = (now.astype(f32) + tail(before_node, ns_buf[...])).astype(bf16)
     nodes_out[...] = updated
     picked = dot(oh_lists[...], updated)
@@ -226,19 +270,15 @@
         picked = jnp.where(place < 4, picked[:, :half], picked[:, half:])
     outgoing[...] = picked.astype(bf16)
     if not last:
-
-        def drain(b, carry):
+        for b in range(blocks):
             c_fresh(b).wait()
-            return carry
-
-        lax.fori_loop(0, live_blocks, drain, 0)
-
-
-def run_layer(layer, last, live, send, recv_rows, lists, incoming, before, edges, nodes, ef, es, nf, ns):
+
+
+def run_layer(layer, last, send, recv, lists, incoming, before, edges, nodes, ef, es, nf, ns):
     count, width = nodes.shape
     edge_count = edges.shape[0]
     blocks = edge_count // BLOCK
-    out_rows = lists.shape[0] * 128
+    out_rows = lists.shape[1] * 8
     vm = pl.BlockSpec(memory_space=VMEM)
     hb = pl.BlockSpec(memory_space=HBM)
     out_shape = [
@@ -253,37 +293,43 @@
         scratch += [VMEM((edge_count, width), bf16), VMEM((edge_count, width), bf16), pltpu.SemaphoreType.DMA((blocks,))]
     scratch += [
         VMEM((width, width), bf16),
-        VMEM((edge_count, width), f32),
+        VMEM((edge_count, width), bf16),
         VMEM((width, width), bf16),
         VMEM((count, width), bf16),
         VMEM((2 * width, width), bf16),
         VMEM((width, width), bf16),
         VMEM(incoming.shape, bf16),
-        VMEM((BLOCK, incoming.shape[0]), bf16),
+        VMEM((3, SUB, incoming.shape[0]), bf16),
+        VMEM((2, SUB, width), f32),
         VMEM((out_rows, count), bf16),
         VMEM((count, width), f32),
+        VMEM((out_rows, 128), f32),
+        VMEM((SUB, width), bf16),
+        VMEM((SUB, width), f32),
+        VMEM((SUB, width), bf16),
+        VMEM((count, SUB), bf16),
         pltpu.SemaphoreType.DMA((6,)),
         pltpu.SemaphoreType.DMA((2, blocks)),
     ]
     return pl.pallas_call(
         functools.partial(layer_kernel, layer, last),
         out_shape=out_shape,
-        in_specs=[pl.BlockSpec(memory_space=pltpu.SMEM), vm, vm, vm, vm] + [hb] * 7,
+        in_specs=[vm] * 4 + [hb] * 7,
         out_specs=out_specs,
         scratch_shapes=scratch,
         compiler_params=pltpu.CompilerParams(vmem_limit_bytes=GRANT),
         cost_estimate=pl.CostEstimate(flops=9 * edge_count * width * width, bytes_accessed=12 << 20, transcendentals=0),
         name=f"layer_{layer}",
-    )(live, send, recv_rows, lists, incoming, before, edges, nodes, ef, es, nf, ns)
+    )(send, recv, lists, incoming, *pinned(before, edges, nodes, ef, es, nf, ns))
 
 
 def decode_before_kernel(edges, grid, first, grid_first, out, out_grid):
     width = grid.shape[1]
     cells = grid.shape[0]
-    out_grid[...] = dot(grid[...], grid_first[...])
+    out_grid[...] = (0.5 * dot(grid[...], grid_first[...])).astype(bf16)
     rows = edges[...].reshape(3 * cells, width)
     own = dot(rows, first[:width, :]).reshape(3, cells, width)
-    out[...] = own + dot(grid[...], first[2 * width :, :])[None]
+    out[...] = (0.5 * (own + dot(grid[...], first[2 * width :, :])[None])).astype(bf16)
 
 
 def decode_before(edges, grid, first, grid_first):
@@ -303,8 +349,8 @@
             pl.BlockSpec((CELLS, width), lambda i: (i, 0)),
         ],
         out_shape=[
-            jax.ShapeDtypeStruct((3, cells, width), f32),
-            jax.ShapeDtypeStruct((cells, width), f32),
+            jax.ShapeDtypeStruct((3, cells, width), bf16),
+            jax.ShapeDtypeStruct((cells, width), bf16),
         ],
         compiler_params=pltpu.CompilerParams(vmem_limit_bytes=GRANT),
         cost_estimate=pl.CostEstimate(flops=10 * cells * width * width, bytes_accessed=14 << 20, transcendentals=0),
@@ -314,7 +360,7 @@
 
 def decode_kernel(
     sources, incoming, before, before_grid, grid, first, second, grid_first, grid_second, out,
-    mid_buf, before_buf, bg_buf, grid_buf, second_buf, gf_buf, gs_buf, table, oh, out_buf, sem, bsem, osem,
+    mid_buf, before_buf, bg_buf, grid_buf, second_buf, gf_buf, gs_buf, table, oh, ready, summed, hidden, raw, ready_cells, hidden_cells, raw_cells, out_buf, sem, bsem, osem,
 ):
     width = grid.shape[1]
     cells = grid.shape[0]
@@ -364,34 +410,71 @@
     left = left.reshape(cells // 2, half).astype(bf16)
     right = right.reshape(cells // 2, half).astype(bf16)
     c_mid.wait()
-    table[...] = (dot(left, mid_buf[:half, :]) + dot(right, mid_buf[half:, :])).astype(bf16)
+    table[...] = (0.5 * (dot(left, mid_buf[:half, :]) + dot(right, mid_buf[half:, :]))).astype(bf16)
     c_second.wait()
     c_gf.wait()
     c_gs.wait()
+    c_before(0).wait()
     steps = CELLS // 128
-
-    def advance(b, carry):
-        rows = pl.ds(pl.multiple_of(b * CELLS, CELLS), CELLS)
-        c_before(b).wait()
-        summed = jnp.zeros((CELLS, width), f32)
-        for branch in range(3):
-            fill_picker(oh.at[branch], sources, branch * (cells // 128) + b * steps, CELLS, table.shape[0], 0)
-            result = tail(dot(oh[branch], table[...]) + before_buf[branch, rows, :], second_buf[...])
-            summed = summed + result.astype(bf16).astype(f32)
+    items = [(b, branch) for b in range(blocks) for branch in range(3)]
+
+    def picker(i):
+        b, branch = items[i]
+        fill_picker(oh.at[i % 3], sources, branch * (cells // 128) + b * steps, CELLS, table.shape[0], 0)
+
+    def first_half(i, part):
+        columns = slice(part * half, (part + 1) * half)
+        ready[i % 2, :, columns] = dot(oh[i % 3], table[:, columns])
+
+    def hide(i):
+        b, branch = items[i]
+        for c in range(0, CELLS, CHUNK):
+            rows = slice(b * CELLS + c, b * CELLS + c + CHUNK)
+            value = ready[i % 2, c : c + CHUNK, :] + before_buf[branch, rows, :].astype(f32)
+            hidden[c : c + CHUNK, :] = silu_of_double(value).astype(bf16)
+
+    def finish(i):
+        branch = items[i][1]
+        for c in range(0, CELLS, CHUNK):
+            rows = slice(c, c + CHUNK)
+            result = normalize(raw[rows, :]).astype(bf16).astype(f32)
+            summed[rows, :] = result if branch == 0 else summed[rows, :] + result
+
+    def finish_cells(b):
         c_bg(b).wait()
         c_grid(b).wait()
-        result = tail(dot(summed.astype(bf16), gf_buf[...]) + bg_buf[rows, :], gs_buf[...])
-        out_buf[rows, :] = (grid_buf[rows, :].astype(f32) + result).astype(bf16)
+        ready_cells[...] = dot(summed[...].astype(bf16), gf_buf[...])
+        for c in range(0, CELLS, CHUNK):
+            rows = slice(b * CELLS + c, b * CELLS + c + CHUNK)
+            value = 0.5 * ready_cells[c : c + CHUNK, :] + bg_buf[rows, :].astype(f32)
+            hidden_cells[c : c + CHUNK, :] = silu_of_double(value).astype(bf16)
+        raw_cells[...] = dot(hidden_cells[...], gs_buf[...])
+        for c in range(0, CELLS, CHUNK):
+            rows = slice(b * CELLS + c, b * CELLS + c + CHUNK)
+            result = normalize(raw_cells[c : c + CHUNK, :])
+            out_buf[rows, :] = (grid_buf[rows, :].astype(f32) + result).astype(bf16)
         c_out(b).start()
-        return carry
-
-    lax.fori_loop(0, blocks, advance, 0)
-
-    def drain(b, carry):
+
+    picker(0)
+    picker(1)
+    first_half(0, 0)
+    first_half(0, 1)
+    for i, (b, branch) in enumerate(items):
+        if branch == 2 and b + 1 < blocks:
+            c_before(b + 1).wait()
+        if i + 2 < len(items):
+            picker(i + 2)
+        hide(i)
+        if i + 1 < len(items):
+            first_half(i + 1, 0)
+        raw[...] = dot(hidden[...], second_buf[...])
+        if i + 1 < len(items):
+            first_half(i + 1, 1)
+        finish(i)
+        if branch == 2:
+            finish_cells(b)
+    for b in range(blocks):
         c_out(b).wait()
-        return carry
-
-    lax.fori_loop(0, blocks, drain, 0)
 
 
 def decode(sources, incoming, before, before_grid, grid, first, second, grid_first, grid_second):
@@ -405,14 +488,21 @@
         out_specs=hb,
         scratch_shapes=[
             VMEM((width, width), bf16),
-            VMEM((3, cells, width), f32),
-            VMEM((cells, width), f32),
+            VMEM((3, cells, width), bf16),
+            VMEM((cells, width), bf16),
             VMEM((cells, width), bf16),
             VMEM((width, width), bf16),
             VMEM((width, width), bf16),
             VMEM((width, width), bf16),
             VMEM((incoming.shape[0] // 2, width), bf16),
             VMEM((3, CELLS, incoming.shape[0] // 2), bf16),
+            VMEM((2, CELLS, width), f32),
+            VMEM((CELLS, width), f32),
+            VMEM((CELLS, width), bf16),
+            VMEM((CELLS, width), f32),
+            VMEM((CELLS, width), f32),
+            VMEM((CELLS, width), bf16),
+            VMEM((CELLS, width), f32),
             VMEM((cells, width), bf16),
             pltpu.SemaphoreType.DMA((5,)),
             pltpu.SemaphoreType.DMA((3, blocks)),
@@ -421,7 +511,7 @@
         compiler_params=pltpu.CompilerParams(vmem_limit_bytes=GRANT),
         cost_estimate=pl.CostEstimate(flops=16 * cells * width * width, bytes_accessed=13 << 20, transcendentals=0),
         name="decode",
-    )(sources, incoming, before, before_grid, grid, first, second, grid_first, grid_second)
+    )(sources, incoming, *pinned(before, before_grid, grid, first, second, grid_first, grid_second))
 
 
 def exchange(rows):
@@ -450,25 +540,21 @@
 ):
     tile_lat, tile_lon, width = grid_state.shape
     cells = tile_lat * tile_lon
-    halo = halo_lists.reshape(-1, 128)
+    halo = halo_lists.reshape(halo_lists.shape[1:]).T
     outgoing = pick_first(halo, mesh_nodes)
     incoming = exchange(outgoing)
-    live = (jnp.sum((edge_recv >= 0).astype(jnp.int32)) + (BLOCK - 1)) // BLOCK
-    live = live.reshape(1)
     send = edge_send.reshape(-1, 128)
     recv = edge_recv.reshape(-1, 128)
-    recv_rows = edge_recv.reshape(-1, BLOCK)
-    decoder_rows = decoder_lists.reshape(decoder_lists.shape[1], decoder_lists.shape[2])
-    decoder_rows = jnp.concatenate([decoder_rows, decoder_rows], axis=1).reshape(-1, 128)
+    decoder_rows = decoder_lists.reshape(decoder_lists.shape[1:]).T
     grid = grid_state.reshape(cells, width)
     sources = decoder_sources.reshape(-1, 128)
     nodes, edges = mesh_nodes, mesh_edges
     layers = edge_first.shape[0]
     for layer in range(layers):
         last = layer == layers - 1
-        before = edges_before(live, edges, send, recv, nodes, edge_first, layer)
+        before = edges_before(edges, send, recv, nodes, edge_first, layer)
         results = run_layer(
-            layer, last, live, send, recv_rows, decoder_rows if last else halo, incoming, before, edges, nodes,
+            layer, last, send, recv, decoder_rows if last else halo, incoming, before, edges, nodes,
             edge_first, edge_second, node_first, node_second,
         )
         nodes, outgoing = results[:2]

time: 121 us -> 111 us (0.917)
  starting transfers between devices: 31.5 us -> 20.8 us
  local copies, waits for them, and re-layouts: 6.3 us -> 16.7 us
  waiting for transfers between devices: 32.4 us -> 22.4 us
    unnamed x13 -> x44, local copies, waits for them, and re-layouts: 3.57 us -> 16.6 us
    all_to_all x3, starting transfers between devices: 31.5 us -> 20.8 us  [exchange(): lax.all_to_all(chunks, ('lat', 'lon'), split_axis=0, concat_axis=0, tiled...]
    all_to_all x3, waiting for transfers between devices: 32.4 us -> 22.4 us  [exchange(): lax.all_to_all(chunks, ('lat', 'lon'), split_axis=0, concat_axis=0, tiled...]
    pallas_call x2, Pallas kernels: 14.7 us -> 22.2 us  [run_layer(): pl.pallas_call(functools.partial(layer_kernel, layer, last), out_shape=ou...]
    pallas_call x1, Pallas kernels: 15.6 us -> 11.4 us  [decode(): pl.pallas_call(decode_kernel, out_shape=jax.ShapeDtypeStruct((cells, widt...]
    pallas_call x1, Pallas kernels: 8.03 us -> 4.09 us  [decode_before(): pl.pallas_call(decode_before_kernel, grid=(cells // CELLS,), in_specs=[pl...]
    pallas_call x2, Pallas kernels: 8.24 us -> 10.5 us  [edges_before(): pl.pallas_call(before_kernel, grid_spec=grid_spec, out_shape=jax.ShapeDty...]
    reshape x3 -> x0, local copies, waits for them, and re-layouts: 1.96 us -> none  [the longest x1 0.68 us: shards(): halo = halo_lists.reshape(-1, 128)]
  transfers between devices with their start and end apart: 3 -> 3, of which waited for: 3 -> 3; matrix products, arithmetic and copies ran while one was open for 2% -> 0% of each run, Pallas kernels for 13% -> 13%
where the time goes in v2:
time: 111 us
  Pallas kernels  49.8 us (45%)
  waiting for transfers between devices  22.4 us (20%)
  starting transfers between devices  20.8 us (19%)
  local copies, waits for them, and re-layouts  16.7 us (15%)
    all_to_all x3, waiting for transfers between devices, exchange(): lax.all_to_all(chunks, ('lat', 'lon'), split_axis=0, concat_axis=0, tiled...  22.4 us
    pallas_call x2, Pallas kernels, run_layer(): pl.pallas_call(functools.partial(layer_kernel, layer, last), out_shape=ou...  22.2 us
    all_to_all x3, starting transfers between devices, exchange(): lax.all_to_all(chunks, ('lat', 'lon'), split_axis=0, concat_axis=0, tiled...  20.8 us
    unnamed x44, local copies, waits for them, and re-layouts  16.6 us
    pallas_call x1, Pallas kernels, decode(): pl.pallas_call(decode_kernel, out_shape=jax.ShapeDtypeStruct((cells, widt...  11.4 us
    pallas_call x2, Pallas kernels, edges_before(): pl.pallas_call(before_kernel, grid_spec=grid_spec, out_shape=jax.ShapeDty...  10.5 us
    pallas_call x1, Pallas kernels, decode_before(): pl.pallas_call(decode_before_kernel, grid=(cells // CELLS,), in_specs=[pl...  4.09 us
  transfers between devices with their start and end apart: 3, of which 3 were waited for; matrix products, arithmetic and copies ran while one was open for 0% of the time, Pallas kernels for 13%

profile of v2, /device:TPU:1, one launch (start us, length us, event | category | flops | bytes accessed | tf_op | source)
XLA Modules:
  0.0 110.7 jit_solution(12911800940818494677)
XLA Ops:
  0.6 0.0 copy-start
  0.6 0.9 copy-done
  1.6 0.7 copy-done.2
  2.3 0.0 copy-start.1
  2.3 0.0 copy-start.7
  2.3 0.0 copy-start.11
  2.3 1.6 %pick_first.1 = bf16[1024,512]{1,0:T(8,128)(2,1)} custom-call(s32[8,128]{1,0:T(8,128)S(1)} %bitcast.20, bf16[256,512]{1,0:T(8,128)(2,1)S(1)} %copy-done), custom_call_target="tpu_custom_call" | custom-call | flops 268435456 | bytes 1048576 | tf_op jit(solution)/shard_map/pick_first/pallas_call | solution.py:80
  3.9 11.5 %all-to-all-start = ((bf16[128,8,512]{2,1,0:T(8,128)(2,1)}), bf16[128,8,512]{2,1,0:T(8,128)(2,1)S(1)}, u32[]{:S(2)}, u32[]{:S(2)}) async-start(bf16[128,8,512]{2,1,0:T(8,128)(2,1)} %bitcast.7), calls=%async_computation | async-start | bytes 2097152 | tf_op jit(solution)/shard_map/all_to_all | solution.py:519
  15.4 0.0 copy-done.1
  15.4 0.0 copy-done.7
  15.4 0.0 copy-done.11
  15.4 0.0 copy-done.12
  15.4 0.0 copy-start.4
  15.5 1.9 %copy-done.4 = bf16[2,1536,512]{2,1,0:T(8,128)(2,1)S(1)} copy-done((bf16[2,1536,512]{2,1,0:T(8,128)(2,1)S(1)}, bf16[2,1536,512]{2,1,0:T(8,128)(2,1)}, u32[]{:S(2)}) %copy-start.4) | copy-done | bytes 3145752
  17.3 5.2 %edges_before_0.1.before = bf16[2048,512]{1,0:T(8,128)(2,1)S(1)} custom-call(bf16[2048,512]{1,0:T(8,128)(2,1)S(1)} %copy-done.7, s32[16,128]{1,0:T(8,128)S(1)} %bitcast.25, s32[16,128]{1,0:T(8,128)S(1)} %bitcast.29, bf16[256,512]{1,0:T(8,128)(2,1)S(1)} %copy-done.1, bf16[2,1536,512]{2,1,0:T(8,128)(2,1)S(1)} %copy-done.4), custom_call_target="tpu_custom_call" | custom-call | flops 4294967296 | bytes 8388608 | tf_op jit(solution)/shard_map/edges_before_0/pallas_call | solution.py:126
  22.6 0.0 copy-start.18
  22.6 1.3 %copy-done.18 = bf16[2048,512]{1,0:T(8,128)(2,1)} copy-done((bf16[2048,512]{1,0:T(8,128)(2,1)}, bf16[2048,512]{1,0:T(8,128)(2,1)S(1)}, u32[]{:S(2)}) %copy-start.18) | copy-done | bytes 2097176
  23.9 10.4 %all-to-all-done = bf16[128,8,512]{2,1,0:T(8,128)(2,1)S(1)} async-done(((bf16[128,8,512]{2,1,0:T(8,128)(2,1)}), bf16[128,8,512]{2,1,0:T(8,128)(2,1)S(1)}, u32[]{:S(2)}, u32[]{:S(2)}) %all-to-all-start) | async-done | bytes 1048608 | tf_op jit(solution)/shard_map/all_to_all | solution.py:519
  34.3 0.0 copy-done.3
  34.3 12.1 %layer_0.1 = (bf16[256,512]{1,0:T(8,128)(2,1)S(1)}, bf16[1024,512]{1,0:T(8,128)(2,1)}, bf16[2048,512]{1,0:T(8,128)(2,1)S(1)}) custom-call(s32[16,128]{1,0:T(8,128)S(1)} %bitcast.26, s32[16,128]{1,0:T(8,128)S(1)} %bitcast.30, s32[8,128]{1,0:T(8,128)S(1)} %bitcast.21, bf16[1024,512]{1,0:T(8,128)(2,1)S(1)} %bitcast.18, bf16[2048,512]{1,0:T(8,128)(2,1)} %copy-done.18, ...), custom_call_target="tpu_custom_call" | custom-call | flops 4831838208 | bytes 12582912 | tf_op jit(solution)/shard_map/layer_0/pallas_call | solution.py:314
  46.5 0.0 copy-start.16
  46.5 0.0 copy-start.20
  46.5 4.7 %all-to-all-start.1 = ((bf16[128,8,512]{2,1,0:T(8,128)(2,1)}), bf16[128,8,512]{2,1,0:T(8,128)(2,1)S(1)}, u32[]{:S(2)}, u32[]{:S(2)}) async-start(bf16[128,8,512]{2,1,0:T(8,128)(2,1)} %bitcast.9), calls=%async_computation.1 | async-start | bytes 2097152 | tf_op jit(solution)/shard_map/all_to_all | solution.py:519
  51.2 0.0 copy-done.16
  51.2 0.0 copy-start.5
  51.2 1.9 %copy-done.5 = bf16[2,1536,512]{2,1,0:T(8,128)(2,1)S(1)} copy-done((bf16[2,1536,512]{2,1,0:T(8,128)(2,1)S(1)}, bf16[2,1536,512]{2,1,0:T(8,128)(2,1)}, u32[]{:S(2)}) %copy-start.5) | copy-done | bytes 3145752
  53.1 1.6 %copy-done.17 = bf16[2048,512]{1,0:T(8,128)(2,1)S(1)} copy-done((bf16[2048,512]{1,0:T(8,128)(2,1)S(1)}, bf16[2048,512]{1,0:T(8,128)(2,1)}, u32[]{:S(2)}) %copy-start.17) | copy-done | bytes 2097176
  54.6 5.2 %edges_before_1.1.before = bf16[2048,512]{1,0:T(8,128)(2,1)S(1)} custom-call(bf16[2048,512]{1,0:T(8,128)(2,1)S(1)} %copy-done.17, s32[16,128]{1,0:T(8,128)S(1)} %bitcast.27, s32[16,128]{1,0:T(8,128)S(1)} %bitcast.31, bf16[256,512]{1,0:T(8,128)(2,1)S(1)} %get-tuple-element.11.nodes, bf16[2,1536,512]{2,1,0:T(8,128)(2,1)S(1)} %copy-done.5), custom_call_target="tpu_custom_call" | custom-call | flops 4294967296 | bytes 8388608 | tf_op jit(solution)/shard_map/edges_before_1/pallas_call | solution.py:126
  59.9 0.0 copy-done.20
  59.9 0.0 copy-start.19
  59.9 1.3 %copy-done.19 = bf16[2048,512]{1,0:T(8,128)(2,1)} copy-done((bf16[2048,512]{1,0:T(8,128)(2,1)}, bf16[2048,512]{1,0:T(8,128)(2,1)S(1)}, u32[]{:S(2)}) %copy-start.19) | copy-done | bytes 2097176
  61.2 9.0 %all-to-all-done.1 = bf16[128,8,512]{2,1,0:T(8,128)(2,1)S(1)} async-done(((bf16[128,8,512]{2,1,0:T(8,128)(2,1)}), bf16[128,8,512]{2,1,0:T(8,128)(2,1)S(1)}, u32[]{:S(2)}, u32[]{:S(2)}) %all-to-all-start.1) | async-done | bytes 1048608 | tf_op jit(solution)/shard_map/all_to_all | solution.py:519
  70.2 0.0 copy-done.13
  70.2 10.0 %layer_1.1 = (bf16[256,512]{1,0:T(8,128)(2,1)}, bf16[1024,256]{1,0:T(8,128)(2,1)}) custom-call(s32[16,128]{1,0:T(8,128)S(1)} %bitcast.28, s32[16,128]{1,0:T(8,128)S(1)} %bitcast.32, s32[4,128]{1,0:T(4,128)S(1)} %bitcast.33, bf16[1024,512]{1,0:T(8,128)(2,1)S(1)} %bitcast.17, bf16[2048,512]{1,0:T(8,128)(2,1)} %copy-done.19, bf16[2048,512]{1,0:T(8,128)(2,1)} %copy-done.16, ...), custom_call_target="tpu_custom_call" | custom-call | flops 4831838208 | bytes 12582912 | tf_op jit(solution)/shard_map/layer_1/pallas_call | solution.py:314
  80.2 4.6 %all-to-all-start.2 = ((bf16[128,8,256]{2,1,0:T(8,128)(2,1)}), bf16[128,8,256]{2,1,0:T(8,128)(2,1)S(1)}, u32[]{:S(2)}, u32[]{:S(2)}) async-start(bf16[128,8,256]{2,1,0:T(8,128)(2,1)} %bitcast.11), calls=%async_computation.2 | async-start | bytes 1048576 | tf_op jit(solution)/shard_map/all_to_all | solution.py:519
  84.8 0.0 copy-done.21
  84.9 0.1 reshape.54.sources
  84.9 0.0 copy-done.8
  84.9 0.0 copy-start.6
  85.0 1.9 %copy-done.6 = bf16[3,32,32,512]{3,2,1,0:T(8,128)(2,1)S(1)} copy-done((bf16[3,32,32,512]{3,2,1,0:T(8,128)(2,1)S(1)}, bf16[3,32,32,512]{3,2,1,0:T(8,128)(2,1)}, u32[]{:S(2)}) %copy-start.6) | copy-done | bytes 3145752
  86.8 1.2 %copy-done.9 = bf16[32,32,512]{2,1,0:T(8,128)(2,1)S(1)} copy-done((bf16[32,32,512]{2,1,0:T(8,128)(2,1)S(1)}, bf16[32,32,512]{2,1,0:T(8,128)(2,1)}, u32[]{:S(2)}) %copy-start.9) | copy-done | bytes 1048600
  88.1 1.2 %copy-done.10 = bf16[1024,512]{1,0:T(8,128)(2,1)S(1)} copy-done((bf16[1024,512]{1,0:T(8,128)(2,1)S(1)}, bf16[1024,512]{1,0:T(8,128)(2,1)}, u32[]{:S(2)}) %copy-start.10) | copy-done | bytes 1048600
  89.3 4.1 %decode_before.1 = (bf16[3,1024,512]{2,1,0:T(8,128)(2,1)S(1)}, bf16[1024,512]{1,0:T(8,128)(2,1)S(1)}) custom-call(bf16[3,1024,512]{2,1,0:T(8,128)(2,1)S(1)} %bitcast.22, bf16[1024,512]{1,0:T(8,128)(2,1)S(1)} %bitcast.24, bf16[1536,512]{1,0:T(8,128)(2,1)S(1)} %copy-done.8, bf16[1024,512]{1,0:T(8,128)(2,1)S(1)} %copy-done.10), custom_call_target="tpu_custom_call" | custom-call | flops 2684354560 | bytes 14680064 | tf_op jit(solution)/shard_map/decode_before/pallas_call | solution.py:338
  93.4 0.0 copy-start.14
  93.4 1.6 %copy-done.14 = bf16[3,1024,512]{2,1,0:T(8,128)(2,1)} copy-done((bf16[3,1024,512]{2,1,0:T(8,128)(2,1)}, bf16[3,1024,512]{2,1,0:T(8,128)(2,1)S(1)}, u32[]{:S(2)}) %copy-start.14) | copy-done | bytes 3145752
  95.0 1.0 copy-done.15
  96.0 3.1 %all-to-all-done.2 = bf16[128,8,256]{2,1,0:T(8,128)(2,1)S(1)} async-done(((bf16[128,8,256]{2,1,0:T(8,128)(2,1)}), bf16[128,8,256]{2,1,0:T(8,128)(2,1)S(1)}, u32[]{:S(2)}, u32[]{:S(2)}) %all-to-all-start.2) | async-done | bytes 524320 | tf_op jit(solution)/shard_map/all_to_all | solution.py:519
  99.0 11.4 %decode.1 = bf16[1024,512]{1,0:T(8,128)(2,1)} custom-call(s32[24,128]{1,0:T(8,128)S(1)} %reshape.54.sources, bf16[1024,256]{1,0:T(8,128)(2,1)S(1)} %bitcast.19, bf16[3,1024,512]{2,1,0:T(8,128)(2,1)} %copy-done.14, bf16[1024,512]{1,0:T(8,128)(2,1)} %copy-done.15, bf16[1024,512]{1,0:T(8,128)(2,1)} %bitcast.23, bf16[1536,512]{1,0:T(8,128)(2,1)} %first.7, ...), custom_call_target="tpu_custom_call" | custom-call | flops 4294967296 | bytes 13631488 | tf_op jit(solution)/shard_map/decode/pallas_call | solution.py:484
  (10 shorter events, 0.0 us)
Async XLA Ops:
  0.6 1.0 copy-start
  1.6 0.7 copy-start.2
  2.3 13.1 %copy-start.1 = (bf16[256,512]{1,0:T(8,128)(2,1)S(1)}, bf16[256,512]{1,0:T(8,128)(2,1)}, u32[]{:S(2)}) copy-start(bf16[256,512]{1,0:T(8,128)(2,1)} %nodes.5) | copy-start | bytes 786436
  2.3 13.1 %copy-start.7 = (bf16[2048,512]{1,0:T(8,128)(2,1)S(1)}, bf16[2048,512]{1,0:T(8,128)(2,1)}, u32[]{:S(2)}) copy-start(bf16[2048,512]{1,0:T(8,128)(2,1)} %edges.3) | copy-start | bytes 6291460
  2.3 13.2 %copy-start.11 = (s32[2048]{0:T(1024)S(1)}, s32[2048]{0:T(1024)}, u32[]{:S(2)}) copy-start(s32[2048]{0:T(1024)} %param.21) | copy-start | bytes 24580
  2.3 13.2 %copy-start.12 = (s32[2048]{0:T(1024)S(1)}, s32[2048]{0:T(1024)}, u32[]{:S(2)}) copy-start(s32[2048]{0:T(1024)} %param.22) | copy-start | bytes 24580
  3.9 30.4 %all-to-all-start = ((bf16[128,8,512]{2,1,0:T(8,128)(2,1)}), bf16[128,8,512]{2,1,0:T(8,128)(2,1)S(1)}, u32[]{:S(2)}, u32[]{:S(2)}) async-start(bf16[128,8,512]{2,1,0:T(8,128)(2,1)} %bitcast.7), calls=%async_computation | async-start | bytes 2097152 | tf_op jit(solution)/shard_map/all_to_all | solution.py:519
  15.4 1.9 %copy-start.4 = (bf16[2,1536,512]{2,1,0:T(8,128)(2,1)S(1)}, bf16[2,1536,512]{2,1,0:T(8,128)(2,1)}, u32[]{:S(2)}) copy-start(bf16[2,1536,512]{2,1,0:T(8,128)(2,1)} %edge_first.3) | copy-start | bytes 9437188
  17.3 17.0 %copy-start.3 = (s32[1,128,8]{1,2,0:T(8,128)S(1)}, s32[1,128,8]{1,2,0:T(8,128)}, u32[]{:S(2)}) copy-start(s32[1,128,8]{1,2,0:T(8,128)} %param.23) | copy-start | bytes 12292
  22.6 1.4 %copy-start.18 = (bf16[2048,512]{1,0:T(8,128)(2,1)}, bf16[2048,512]{1,0:T(8,128)(2,1)S(1)}, u32[]{:S(2)}) copy-start(bf16[2048,512]{1,0:T(8,128)(2,1)S(1)} %edges_before_0.1.before) | copy-start | bytes 6291460
  46.5 4.7 %copy-start.16 = (bf16[2048,512]{1,0:T(8,128)(2,1)}, bf16[2048,512]{1,0:T(8,128)(2,1)S(1)}, u32[]{:S(2)}) copy-start(bf16[2048,512]{1,0:T(8,128)(2,1)S(1)} %get-tuple-element.10.edges) | copy-start | bytes 6291460
  46.5 13.4 %copy-start.20 = (bf16[256,512]{1,0:T(8,128)(2,1)}, bf16[256,512]{1,0:T(8,128)(2,1)S(1)}, u32[]{:S(2)}) copy-start(bf16[256,512]{1,0:T(8,128)(2,1)S(1)} %get-tuple-element.11.nodes) | copy-start | bytes 786436
  46.5 23.7 %all-to-all-start.1 = ((bf16[128,8,512]{2,1,0:T(8,128)(2,1)}), bf16[128,8,512]{2,1,0:T(8,128)(2,1)S(1)}, u32[]{:S(2)}, u32[]{:S(2)}) async-start(bf16[128,8,512]{2,1,0:T(8,128)(2,1)} %bitcast.9), calls=%async_computation.1 | async-start | bytes 2097152 | tf_op jit(solution)/shard_map/all_to_all | solution.py:519
  51.2 1.9 %copy-start.5 = (bf16[2,1536,512]{2,1,0:T(8,128)(2,1)S(1)}, bf16[2,1536,512]{2,1,0:T(8,128)(2,1)}, u32[]{:S(2)}) copy-start(bf16[2,1536,512]{2,1,0:T(8,128)(2,1)} %edge_first.3) | copy-start | bytes 9437188
  53.1 1.6 %copy-start.17 = (bf16[2048,512]{1,0:T(8,128)(2,1)S(1)}, bf16[2048,512]{1,0:T(8,128)(2,1)}, u32[]{:S(2)}) copy-start(bf16[2048,512]{1,0:T(8,128)(2,1)} %copy-done.16) | copy-start | bytes 6291460
  54.6 15.5 %copy-start.13 = (s32[1,128,4]{1,2,0:T(4,128)S(1)}, s32[1,128,4]{1,2,0:T(4,128)}, u32[]{:S(2)}) copy-start(s32[1,128,4]{1,2,0:T(4,128)} %param.24) | copy-start | bytes 6148
  59.9 1.3 %copy-start.19 = (bf16[2048,512]{1,0:T(8,128)(2,1)}, bf16[2048,512]{1,0:T(8,128)(2,1)S(1)}, u32[]{:S(2)}) copy-start(bf16[2048,512]{1,0:T(8,128)(2,1)S(1)} %edges_before_1.1.before) | copy-start | bytes 6291460
  70.2 14.7 %copy-start.21 = (s32[3,32,32]{2,1,0:T(8,128)S(1)}, s32[3,32,32]{2,1,0:T(8,128)}, u32[]{:S(2)}) copy-start(s32[3,32,32]{2,1,0:T(8,128)} %param.25) | copy-start | bytes 36868
  70.2 14.8 %copy-start.8 = (bf16[1536,512]{1,0:T(8,128)(2,1)S(1)}, bf16[1536,512]{1,0:T(8,128)(2,1)}, u32[]{:S(2)}) copy-start(bf16[1536,512]{1,0:T(8,128)(2,1)} %first.7) | copy-start | bytes 4718596
  80.2 18.8 %all-to-all-start.2 = ((bf16[128,8,256]{2,1,0:T(8,128)(2,1)}), bf16[128,8,256]{2,1,0:T(8,128)(2,1)S(1)}, u32[]{:S(2)}, u32[]{:S(2)}) async-start(bf16[128,8,256]{2,1,0:T(8,128)(2,1)} %bitcast.11), calls=%async_computation.2 | async-start | bytes 1048576 | tf_op jit(solution)/shard_map/all_to_all | solution.py:519
  84.9 1.9 %copy-start.6 = (bf16[3,32,32,512]{3,2,1,0:T(8,128)(2,1)S(1)}, bf16[3,32,32,512]{3,2,1,0:T(8,128)(2,1)}, u32[]{:S(2)}) copy-start(bf16[3,32,32,512]{3,2,1,0:T(8,128)(2,1)} %param.20) | copy-start | bytes 9437188
  86.8 1.2 %copy-start.9 = (bf16[32,32,512]{2,1,0:T(8,128)(2,1)S(1)}, bf16[32,32,512]{2,1,0:T(8,128)(2,1)}, u32[]{:S(2)}) copy-start(bf16[32,32,512]{2,1,0:T(8,128)(2,1)} %param.19) | copy-start | bytes 3145732
  88.1 1.2 %copy-start.10 = (bf16[1024,512]{1,0:T(8,128)(2,1)S(1)}, bf16[1024,512]{1,0:T(8,128)(2,1)}, u32[]{:S(2)}) copy-start(bf16[1024,512]{1,0:T(8,128)(2,1)} %grid_first.3) | copy-start | bytes 3145732
  93.4 1.6 %copy-start.14 = (bf16[3,1024,512]{2,1,0:T(8,128)(2,1)}, bf16[3,1024,512]{2,1,0:T(8,128)(2,1)S(1)}, u32[]{:S(2)}) copy-start(bf16[3,1024,512]{2,1,0:T(8,128)(2,1)S(1)} %get-tuple-element.14.before) | copy-start | bytes 9437188
  95.0 1.0 copy-start.15

commit v3 on v2

--- a/solution.py
+++ b/solution.py
@@ -13,6 +13,7 @@
 CHUNK = 32
 CELLS = 256
 GRANT = 40 << 20
+FULL = 62 << 20
 bf16 = jnp.bfloat16
 f32 = jnp.float32
 HBM = pltpu.HBM
@@ -83,7 +84,7 @@
         in_specs=[pl.BlockSpec(memory_space=VMEM)] * 2,
         out_specs=pl.BlockSpec(memory_space=VMEM),
         scratch_shapes=[VMEM((rows, nodes.shape[0]), bf16), VMEM((rows, 128), f32)],
-        compiler_params=pltpu.CompilerParams(vmem_limit_bytes=GRANT),
+        compiler_params=pltpu.CompilerParams(vmem_limit_bytes=FULL),
         cost_estimate=pl.CostEstimate(
             flops=2 * rows * nodes.shape[0] * nodes.shape[1], bytes_accessed=1 << 20, transcendentals=0
         ),
@@ -352,7 +353,7 @@
             jax.ShapeDtypeStruct((3, cells, width), bf16),
             jax.ShapeDtypeStruct((cells, width), bf16),
         ],
-        compiler_params=pltpu.CompilerParams(vmem_limit_bytes=GRANT),
+        compiler_params=pltpu.CompilerParams(vmem_limit_bytes=FULL),
         cost_estimate=pl.CostEstimate(flops=10 * cells * width * width, bytes_accessed=14 << 20, transcendentals=0),
         name="decode_before",
     )(edges, grid, first, grid_first)
@@ -412,8 +413,6 @@
     c_mid.wait()
     table[...] = (0.5 * (dot(left, mid_buf[:half, :]) + dot(right, mid_buf[half:, :]))).astype(bf16)
     c_second.wait()
-    c_gf.wait()
-    c_gs.wait()
     c_before(0).wait()
     steps = CELLS // 128
     items = [(b, branch) for b in range(blocks) for branch in range(3)]
@@ -441,6 +440,9 @@
             summed[rows, :] = result if branch == 0 else summed[rows, :] + result
 
     def finish_cells(b):
+        if b == 0:
+            c_gf.wait()
+            c_gs.wait()
         c_bg(b).wait()
         c_grid(b).wait()
         ready_cells[...] = dot(summed[...].astype(bf16), gf_buf[...])

time: 111 us -> 112 us (level)
  local copies, waits for them, and re-layouts: 16.7 us -> 11 us
  Pallas kernels: 49.8 us -> 53.8 us
  waiting for transfers between devices: 22.4 us -> 24.6 us
    unnamed x44 -> x28, local copies, waits for them, and re-layouts: 16.6 us -> 10.9 us
    pallas_call x1, Pallas kernels: 4.09 us -> 7.26 us  [decode_before(): pl.pallas_call(decode_before_kernel, grid=(cells // CELLS,), in_specs=[pl...]
    all_to_all x3, waiting for transfers between devices: 22.4 us -> 24.6 us  [exchange(): lax.all_to_all(chunks, ('lat', 'lon'), split_axis=0, concat_axis=0, tiled...]
  transfers between devices with their start and end apart: 3 -> 3, of which waited for: 3 -> 3; matrix products, arithmetic and copies ran while one was open for 0% -> 0% of each run, Pallas kernels for 13% -> 16%
where the time goes in v3:
time: 112 us; the launch traced here: 111 us
  Pallas kernels  53.8 us (48%)
  waiting for transfers between devices  24.6 us (22%)
  starting transfers between devices  20.7 us (18%)
  local copies, waits for them, and re-layouts  11 us (10%)
    all_to_all x3, waiting for transfers between devices, exchange(): lax.all_to_all(chunks, ('lat', 'lon'), split_axis=0, concat_axis=0, tiled...  24.6 us
    pallas_call x2, Pallas kernels, run_layer(): pl.pallas_call(functools.partial(layer_kernel, layer, last), out_shape=ou...  22.1 us
    all_to_all x3, starting transfers between devices, exchange(): lax.all_to_all(chunks, ('lat', 'lon'), split_axis=0, concat_axis=0, tiled...  20.7 us
    pallas_call x1, Pallas kernels, decode(): pl.pallas_call(decode_kernel, out_shape=jax.ShapeDtypeStruct((cells, widt...  11.3 us
    unnamed x28, local copies, waits for them, and re-layouts  10.9 us
    pallas_call x2, Pallas kernels, edges_before(): pl.pallas_call(before_kernel, grid_spec=grid_spec, out_shape=jax.ShapeDty...  10.5 us
    pallas_call x1, Pallas kernels, decode_before(): pl.pallas_call(decode_before_kernel, grid=(cells // CELLS,), in_specs=[pl...  7.26 us
    pallas_call x1, Pallas kernels, pick_first(): pl.pallas_call(pick_kernel, out_shape=jax.ShapeDtypeStruct((rows, nodes.s...  2.66 us
  transfers between devices with their start and end apart: 3, of which 3 were waited for; matrix products, arithmetic and copies ran while one was open for 0% of the time, Pallas kernels for 16%

profile of v3, /device:TPU:1, one launch (start us, length us, event | category | flops | bytes accessed | tf_op | source)
XLA Modules:
  0.0 111.1 jit_solution(3916599097880038048)
XLA Ops:
  0.6 0.0 copy-start
  0.6 0.0 copy-start.5
  0.7 0.0 copy-start.6
  0.7 2.7 %pick_first.1 = bf16[1024,512]{1,0:T(8,128)(2,1)} custom-call(s32[8,128]{1,0:T(8,128)} %bitcast.20, bf16[256,512]{1,0:T(8,128)(2,1)} %nodes.5), custom_call_target="tpu_custom_call" | custom-call | flops 268435456 | bytes 1048576 | tf_op jit(solution)/shard_map/pick_first/pallas_call | solution.py:81
  3.3 11.5 %all-to-all-start = ((bf16[128,8,512]{2,1,0:T(8,128)(2,1)}), bf16[128,8,512]{2,1,0:T(8,128)(2,1)S(1)}, u32[]{:S(2)}, u32[]{:S(2)}) async-start(bf16[128,8,512]{2,1,0:T(8,128)(2,1)} %bitcast.31), calls=%async_computation | async-start | bytes 2097152 | tf_op jit(solution)/shard_map/all_to_all | solution.py:521
  14.8 0.0 copy-done
  14.8 0.0 copy-done.5
  14.8 0.0 copy-done.6
  14.8 0.0 copy-start.2
  14.9 1.9 %copy-done.2 = bf16[2,1536,512]{2,1,0:T(8,128)(2,1)S(1)} copy-done((bf16[2,1536,512]{2,1,0:T(8,128)(2,1)S(1)}, bf16[2,1536,512]{2,1,0:T(8,128)(2,1)}, u32[]{:S(2)}) %copy-start.2) | copy-done | bytes 3145752
  16.7 0.0 copy-start.4
  16.7 1.6 %copy-done.4 = bf16[2048,512]{1,0:T(8,128)(2,1)S(1)} copy-done((bf16[2048,512]{1,0:T(8,128)(2,1)S(1)}, bf16[2048,512]{1,0:T(8,128)(2,1)}, u32[]{:S(2)}) %copy-start.4) | copy-done | bytes 2097176
  18.3 0.0 copy-start.1
  18.3 5.2 %edges_before_0.1.before = bf16[2048,512]{1,0:T(8,128)(2,1)S(1)} custom-call(bf16[2048,512]{1,0:T(8,128)(2,1)S(1)} %copy-done.4, s32[16,128]{1,0:T(8,128)S(1)} %bitcast.22, s32[16,128]{1,0:T(8,128)S(1)} %bitcast.26, bf16[256,512]{1,0:T(8,128)(2,1)S(1)} %copy-done, bf16[2,1536,512]{2,1,0:T(8,128)(2,1)S(1)} %copy-done.2), custom_call_target="tpu_custom_call" | custom-call | flops 4294967296 | bytes 8388608 | tf_op jit(solution)/shard_map/edges_before_0/pallas_call | solution.py:127
  23.6 0.0 copy-start.10
  23.6 1.3 %copy-done.10 = bf16[2048,512]{1,0:T(8,128)(2,1)} copy-done((bf16[2048,512]{1,0:T(8,128)(2,1)}, bf16[2048,512]{1,0:T(8,128)(2,1)S(1)}, u32[]{:S(2)}) %copy-start.10) | copy-done | bytes 2097176
  24.9 8.8 %all-to-all-done = bf16[128,8,512]{2,1,0:T(8,128)(2,1)S(1)} async-done(((bf16[128,8,512]{2,1,0:T(8,128)(2,1)}), bf16[128,8,512]{2,1,0:T(8,128)(2,1)S(1)}, u32[]{:S(2)}, u32[]{:S(2)}) %all-to-all-start) | async-done | bytes 1048608 | tf_op jit(solution)/shard_map/all_to_all | solution.py:521
  33.7 0.0 copy-done.1
  33.7 12.1 %layer_0.1 = (bf16[256,512]{1,0:T(8,128)(2,1)S(1)}, bf16[1024,512]{1,0:T(8,128)(2,1)}, bf16[2048,512]{1,0:T(8,128)(2,1)S(1)}) custom-call(s32[16,128]{1,0:T(8,128)S(1)} %bitcast.23, s32[16,128]{1,0:T(8,128)S(1)} %bitcast.27, s32[8,128]{1,0:T(8,128)S(1)} %bitcast.21, bf16[1024,512]{1,0:T(8,128)(2,1)S(1)} %bitcast.18, bf16[2048,512]{1,0:T(8,128)(2,1)} %copy-done.10, ...), custom_call_target="tpu_custom_call" | custom-call | flops 4831838208 | bytes 12582912 | tf_op jit(solution)/shard_map/layer_0/pallas_call | solution.py:315
  45.9 0.0 copy-start.8
  45.9 1.3 %copy-done.8 = bf16[2048,512]{1,0:T(8,128)(2,1)} copy-done((bf16[2048,512]{1,0:T(8,128)(2,1)}, bf16[2048,512]{1,0:T(8,128)(2,1)S(1)}, u32[]{:S(2)}) %copy-start.8) | copy-done | bytes 2097176
  47.2 0.0 copy-start.12
  47.2 4.6 %all-to-all-start.1 = ((bf16[128,8,512]{2,1,0:T(8,128)(2,1)}), bf16[128,8,512]{2,1,0:T(8,128)(2,1)S(1)}, u32[]{:S(2)}, u32[]{:S(2)}) async-start(bf16[128,8,512]{2,1,0:T(8,128)(2,1)} %bitcast.9), calls=%async_computation.1 | async-start | bytes 2097152 | tf_op jit(solution)/shard_map/all_to_all | solution.py:521
  51.8 0.0 copy-start.3
  51.8 1.9 %copy-done.3 = bf16[2,1536,512]{2,1,0:T(8,128)(2,1)S(1)} copy-done((bf16[2,1536,512]{2,1,0:T(8,128)(2,1)S(1)}, bf16[2,1536,512]{2,1,0:T(8,128)(2,1)}, u32[]{:S(2)}) %copy-start.3) | copy-done | bytes 3145752
  53.7 0.0 copy-start.9
  53.7 1.6 %copy-done.9 = bf16[2048,512]{1,0:T(8,128)(2,1)S(1)} copy-done((bf16[2048,512]{1,0:T(8,128)(2,1)S(1)}, bf16[2048,512]{1,0:T(8,128)(2,1)}, u32[]{:S(2)}) %copy-start.9) | copy-done | bytes 2097176
  55.3 0.0 copy-start.7
  55.3 5.2 %edges_before_1.1.before = bf16[2048,512]{1,0:T(8,128)(2,1)S(1)} custom-call(bf16[2048,512]{1,0:T(8,128)(2,1)S(1)} %copy-done.9, s32[16,128]{1,0:T(8,128)S(1)} %bitcast.24, s32[16,128]{1,0:T(8,128)S(1)} %bitcast.28, bf16[256,512]{1,0:T(8,128)(2,1)S(1)} %get-tuple-element.11.nodes, bf16[2,1536,512]{2,1,0:T(8,128)(2,1)S(1)} %copy-done.3), custom_call_target="tpu_custom_call" | custom-call | flops 4294967296 | bytes 8388608 | tf_op jit(solution)/shard_map/edges_before_1/pallas_call | solution.py:127
  60.6 0.0 copy-done.12
  60.6 0.0 copy-start.11
  60.6 1.3 %copy-done.11 = bf16[2048,512]{1,0:T(8,128)(2,1)} copy-done((bf16[2048,512]{1,0:T(8,128)(2,1)}, bf16[2048,512]{1,0:T(8,128)(2,1)S(1)}, u32[]{:S(2)}) %copy-start.11) | copy-done | bytes 2097176
  61.9 9.0 %all-to-all-done.1 = bf16[128,8,512]{2,1,0:T(8,128)(2,1)S(1)} async-done(((bf16[128,8,512]{2,1,0:T(8,128)(2,1)}), bf16[128,8,512]{2,1,0:T(8,128)(2,1)S(1)}, u32[]{:S(2)}, u32[]{:S(2)}) %all-to-all-start.1) | async-done | bytes 1048608 | tf_op jit(solution)/shard_map/all_to_all | solution.py:521
  70.9 0.0 copy-done.7
  70.9 0.0 copy-start.13
  70.9 9.9 %layer_1.1 = (bf16[256,512]{1,0:T(8,128)(2,1)}, bf16[1024,256]{1,0:T(8,128)(2,1)}) custom-call(s32[16,128]{1,0:T(8,128)S(1)} %bitcast.25, s32[16,128]{1,0:T(8,128)S(1)} %bitcast.29, s32[4,128]{1,0:T(4,128)S(1)} %bitcast.30, bf16[1024,512]{1,0:T(8,128)(2,1)S(1)} %bitcast.17, bf16[2048,512]{1,0:T(8,128)(2,1)} %copy-done.11, bf16[2048,512]{1,0:T(8,128)(2,1)} %copy-done.8, ...), custom_call_target="tpu_custom_call" | custom-call | flops 4831838208 | bytes 12582912 | tf_op jit(solution)/shard_map/layer_1/pallas_call | solution.py:315
  80.8 4.6 %all-to-all-start.2 = ((bf16[128,8,256]{2,1,0:T(8,128)(2,1)}), bf16[128,8,256]{2,1,0:T(8,128)(2,1)S(1)}, u32[]{:S(2)}, u32[]{:S(2)}) async-start(bf16[128,8,256]{2,1,0:T(8,128)(2,1)} %bitcast.11), calls=%async_computation.2 | async-start | bytes 1048576 | tf_op jit(solution)/shard_map/all_to_all | solution.py:521
  85.4 0.0 copy-done.13
  85.4 0.1 reshape.54.sources
  85.5 7.3 %decode_before.1 = (bf16[3,1024,512]{2,1,0:T(8,128)(2,1)}, bf16[1024,512]{1,0:T(8,128)(2,1)}) custom-call(bf16[3,1024,512]{2,1,0:T(8,128)(2,1)} %bitcast.32, bf16[1024,512]{1,0:T(8,128)(2,1)} %bitcast.33, bf16[1536,512]{1,0:T(8,128)(2,1)} %first.7, bf16[1024,512]{1,0:T(8,128)(2,1)} %grid_first.3), custom_call_target="tpu_custom_call" | custom-call | flops 2684354560 | bytes 14680064 | tf_op jit(solution)/shard_map/decode_before/pallas_call | solution.py:339
  92.8 6.8 %all-to-all-done.2 = bf16[128,8,256]{2,1,0:T(8,128)(2,1)S(1)} async-done(((bf16[128,8,256]{2,1,0:T(8,128)(2,1)}), bf16[128,8,256]{2,1,0:T(8,128)(2,1)S(1)}, u32[]{:S(2)}, u32[]{:S(2)}) %all-to-all-start.2) | async-done | bytes 524320 | tf_op jit(solution)/shard_map/all_to_all | solution.py:521
  99.6 11.3 %decode.1 = bf16[1024,512]{1,0:T(8,128)(2,1)} custom-call(s32[24,128]{1,0:T(8,128)S(1)} %reshape.54.sources, bf16[1024,256]{1,0:T(8,128)(2,1)S(1)} %bitcast.19, bf16[3,1024,512]{2,1,0:T(8,128)(2,1)} %get-tuple-element.14.before, bf16[1024,512]{1,0:T(8,128)(2,1)} %get-tuple-element.15.before_grid, bf16[1024,512]{1,0:T(8,128)(2,1)} %bitcast.34, ...), custom_call_target="tpu_custom_call" | custom-call | flops 4294967296 | bytes 13631488 | tf_op jit(solution)/shard_map/decode/pallas_call | solution.py:486
Async XLA Ops:
  0.6 14.2 %copy-start = (bf16[256,512]{1,0:T(8,128)(2,1)S(1)}, bf16[256,512]{1,0:T(8,128)(2,1)}, u32[]{:S(2)}) copy-start(bf16[256,512]{1,0:T(8,128)(2,1)} %nodes.5) | copy-start | bytes 786436
  0.6 14.2 %copy-start.5 = (s32[2048]{0:T(1024)S(1)}, s32[2048]{0:T(1024)}, u32[]{:S(2)}) copy-start(s32[2048]{0:T(1024)} %param.21) | copy-start | bytes 24580
  0.7 14.2 %copy-start.6 = (s32[2048]{0:T(1024)S(1)}, s32[2048]{0:T(1024)}, u32[]{:S(2)}) copy-start(s32[2048]{0:T(1024)} %param.22) | copy-start | bytes 24580
  3.3 30.4 %all-to-all-start = ((bf16[128,8,512]{2,1,0:T(8,128)(2,1)}), bf16[128,8,512]{2,1,0:T(8,128)(2,1)S(1)}, u32[]{:S(2)}, u32[]{:S(2)}) async-start(bf16[128,8,512]{2,1,0:T(8,128)(2,1)} %bitcast.31), calls=%async_computation | async-start | bytes 2097152 | tf_op jit(solution)/shard_map/all_to_all | solution.py:521
  14.8 1.9 %copy-start.2 = (bf16[2,1536,512]{2,1,0:T(8,128)(2,1)S(1)}, bf16[2,1536,512]{2,1,0:T(8,128)(2,1)}, u32[]{:S(2)}) copy-start(bf16[2,1536,512]{2,1,0:T(8,128)(2,1)} %edge_first.3) | copy-start | bytes 9437188
  16.7 1.6 %copy-start.4 = (bf16[2048,512]{1,0:T(8,128)(2,1)S(1)}, bf16[2048,512]{1,0:T(8,128)(2,1)}, u32[]{:S(2)}) copy-start(bf16[2048,512]{1,0:T(8,128)(2,1)} %edges.3) | copy-start | bytes 6291460
  18.3 15.4 %copy-start.1 = (s32[1,128,8]{1,2,0:T(8,128)S(1)}, s32[1,128,8]{1,2,0:T(8,128)}, u32[]{:S(2)}) copy-start(s32[1,128,8]{1,2,0:T(8,128)} %param.23) | copy-start | bytes 12292
  23.6 1.3 %copy-start.10 = (bf16[2048,512]{1,0:T(8,128)(2,1)}, bf16[2048,512]{1,0:T(8,128)(2,1)S(1)}, u32[]{:S(2)}) copy-start(bf16[2048,512]{1,0:T(8,128)(2,1)S(1)} %edges_before_0.1.before) | copy-start | bytes 6291460
  45.9 1.3 %copy-start.8 = (bf16[2048,512]{1,0:T(8,128)(2,1)}, bf16[2048,512]{1,0:T(8,128)(2,1)S(1)}, u32[]{:S(2)}) copy-start(bf16[2048,512]{1,0:T(8,128)(2,1)S(1)} %get-tuple-element.10.edges) | copy-start | bytes 6291460
  47.2 13.4 %copy-start.12 = (bf16[256,512]{1,0:T(8,128)(2,1)}, bf16[256,512]{1,0:T(8,128)(2,1)S(1)}, u32[]{:S(2)}) copy-start(bf16[256,512]{1,0:T(8,128)(2,1)S(1)} %get-tuple-element.11.nodes) | copy-start | bytes 786436
  47.2 23.7 %all-to-all-start.1 = ((bf16[128,8,512]{2,1,0:T(8,128)(2,1)}), bf16[128,8,512]{2,1,0:T(8,128)(2,1)S(1)}, u32[]{:S(2)}, u32[]{:S(2)}) async-start(bf16[128,8,512]{2,1,0:T(8,128)(2,1)} %bitcast.9), calls=%async_computation.1 | async-start | bytes 2097152 | tf_op jit(solution)/shard_map/all_to_all | solution.py:521
  51.8 1.9 %copy-start.3 = (bf16[2,1536,512]{2,1,0:T(8,128)(2,1)S(1)}, bf16[2,1536,512]{2,1,0:T(8,128)(2,1)}, u32[]{:S(2)}) copy-start(bf16[2,1536,512]{2,1,0:T(8,128)(2,1)} %edge_first.3) | copy-start | bytes 9437188
  53.7 1.6 %copy-start.9 = (bf16[2048,512]{1,0:T(8,128)(2,1)S(1)}, bf16[2048,512]{1,0:T(8,128)(2,1)}, u32[]{:S(2)}) copy-start(bf16[2048,512]{1,0:T(8,128)(2,1)} %copy-done.8) | copy-start | bytes 6291460
  55.3 15.5 %copy-start.7 = (s32[1,128,4]{1,2,0:T(4,128)S(1)}, s32[1,128,4]{1,2,0:T(4,128)}, u32[]{:S(2)}) copy-start(s32[1,128,4]{1,2,0:T(4,128)} %param.24) | copy-start | bytes 6148
  60.6 1.3 %copy-start.11 = (bf16[2048,512]{1,0:T(8,128)(2,1)}, bf16[2048,512]{1,0:T(8,128)(2,1)S(1)}, u32[]{:S(2)}) copy-start(bf16[2048,512]{1,0:T(8,128)(2,1)S(1)} %edges_before_1.1.before) | copy-start | bytes 6291460
  70.9 14.6 %copy-start.13 = (s32[3,32,32]{2,1,0:T(8,128)S(1)}, s32[3,32,32]{2,1,0:T(8,128)}, u32[]{:S(2)}) copy-start(s32[3,32,32]{2,1,0:T(8,128)} %param.25) | copy-start | bytes 36868
  80.8 18.8 %all-to-all-start.2 = ((bf16[128,8,256]{2,1,0:T(8,128)(2,1)}), bf16[128,8,256]{2,1,0:T(8,128)(2,1)S(1)}, u32[]{:S(2)}, u32[]{:S(2)}) async-start(bf16[128,8,256]{2,1,0:T(8,128)(2,1)} %bitcast.11), calls=%async_computation.2 | async-start | bytes 1048576 | tf_op jit(solution)/shard_map/all_to_all | solution.py:521
